TPU v7x, 64 devices: a 2x2x8 block of a 4x4x8 slice. The times are simulated.
64 devices in a mesh: dp: 4 (over x, y), ep: 16 (over z, core).
Axes of the slice: x: 2, y: 2, z: 8, core: 2. Of those that a mesh axis runs over, the one named last changes fastest.
The devices are a block of a 4x4x8 slice.
Arguments:
- tokens: bfloat16 [16384, 2048], P(('dp', 'ep')), parts along dimension 0
- expert_ids: int32 [16384, 8], P(('dp', 'ep')), parts along dimension 0
- gate_vals: float32 [16384, 8], P(('dp', 'ep')), parts along dimension 0
- w_gate: bfloat16 [128, 2048, 768], P('ep')
- w_up: bfloat16 [128, 2048, 768], P('ep')
- w_down: bfloat16 [128, 768, 2048], P('ep')
Outputs:
- output: bfloat16 [16384, 2048], P(('dp', 'ep')), parts along dimension 0
There are 4 independent parts. A program takes and returns all parts, laid end to end along the dimension named above; an argument that names none is the same for every part.
All inputs are finite; a program needn't handle non-finite values.
Results may differ from a plain program's by a relative error of at most 0.0063075.
Values are sent between devices in bfloat16 or wider.
A program may use at most 768 MiB of HBM per device.

v0:
```python
import jax
import jax.numpy as jnp
from jax import lax
from jax.sharding import PartitionSpec as P, NamedSharding


def expert_ffn(expert_in, w_gate, w_up, w_down):
    gate_act = jnp.einsum('lcd,ldf->lcf', expert_in, w_gate, preferred_element_type=jnp.float32)
    up_act = jnp.einsum('lcd,ldf->lcf', expert_in, w_up, preferred_element_type=jnp.float32)
    hidden = (jax.nn.silu(gate_act) * up_act).astype(jnp.bfloat16)
    return jnp.einsum('lcf,lfd->lcd', hidden, w_down, preferred_element_type=jnp.float32).astype(jnp.bfloat16)


def serve_rows(recv_rows, recv_gate, w_gate, w_up, w_down, expert_cap):
    member = recv_gate != 0.0
    exp_slot = jnp.cumsum(member.astype(jnp.int32), axis=0) - 1
    fan_mat = (member.T[:, None, :] & (exp_slot.T[:, None, :] == jnp.arange(expert_cap)[None, :, None])).astype(jnp.bfloat16)
    expert_in = jnp.einsum('lcr,rd->lcd', fan_mat, recv_rows, preferred_element_type=jnp.float32).astype(jnp.bfloat16)
    expert_out = expert_ffn(expert_in, w_gate, w_up, w_down)
    row_outs = jnp.einsum('lcr,lcd->lrd', fan_mat, expert_out, preferred_element_type=jnp.float32)
    dev_sum = jnp.sum(recv_gate.T[:, :, None] * row_outs, axis=0)
    return dev_sum.astype(jnp.bfloat16)


def send_tables(expert_ids, gate_vals, groups, local_count, pair_cap):
    tok_dev = expert_ids.shape[0]
    chosen = jnp.any((expert_ids // local_count)[:, :, None] == jnp.arange(groups)[None, None, :], axis=1)
    send_rank = jnp.cumsum(chosen.astype(jnp.int32), axis=0) - 1
    pack_mask = chosen.T[:, None, :] & (send_rank.T[:, None, :] == jnp.arange(pair_cap)[None, :, None])
    gate_dense = jnp.sum(jnp.where(expert_ids[:, :, None] == jnp.arange(groups * local_count)[None, None, :], gate_vals[:, :, None], 0.0), axis=1)
    gate_t = jnp.swapaxes(gate_dense.reshape(tok_dev, groups, local_count), 0, 1)
    send_gate = jnp.sum(jnp.where(pack_mask[:, :, :, None], gate_t[:, None, :, :], 0.0), axis=2)
    return pack_mask.astype(jnp.bfloat16), send_gate


def solution(mesh):
    groups = mesh.shape['ep']
    row_spec = P(('dp', 'ep'))
    expert_spec = P('ep')

    def device_step(tokens, expert_ids, gate_vals, w_gate, w_up, w_down):
        tok_dev, top_k = expert_ids.shape
        d_model = tokens.shape[1]
        local_count = w_gate.shape[0]
        pair_cap = tok_dev * (top_k // 2) // groups
        expert_cap = tok_dev * top_k // local_count
        row_count = groups * pair_cap
        pack_mat, send_gate = send_tables(expert_ids, gate_vals, groups, local_count, pair_cap)
        send_rows = jnp.einsum('qct,td->qcd', pack_mat, tokens, preferred_element_type=jnp.float32).astype(jnp.bfloat16)
        recv_rows = lax.all_to_all(send_rows, 'ep', 0, 0, tiled=True)
        recv_gate = lax.all_to_all(send_gate, 'ep', 0, 0, tiled=True)
        dev_sum = serve_rows(recv_rows.reshape(row_count, d_model), recv_gate.reshape(row_count, local_count), w_gate, w_up, w_down, expert_cap)
        returned = lax.all_to_all(dev_sum.reshape(groups, pair_cap, d_model), 'ep', 0, 0, tiled=True)
        moe_sum = jnp.einsum('qct,qcd->td', pack_mat, returned, preferred_element_type=jnp.float32)
        return (tokens.astype(jnp.float32) + moe_sum).astype(jnp.bfloat16)

    return jax.shard_map(device_step, mesh=mesh, in_specs=(row_spec, row_spec, row_spec, expert_spec, expert_spec, expert_spec), out_specs=row_spec, check_vma=False)
```

profile of v0, /device:TPU:21, one launch (start us, length us, event | category | flops | bytes accessed | tf_op | source)
XLA Modules:
  0.0 312.8 jit_solution(4489876808615206231)
XLA Ops:
  0.0 0.7 add_select_fusion
  0.7 0.8 copy.36
  1.6 0.6 reduce-window.14
  2.2 0.2 slice_reduce_fusion.1
  2.5 0.8 copy.37
  3.3 1.3 select_reduce_fusion.1
  4.8 1.3 select_reduce_fusion
  6.3 0.7 reshape.69
  7.1 10.7 %all-to-all-start = ((f32[16,1,512]{2,1,0:T(1,128)}), f32[16,1,512]{2,1,0:T(1,128)S(1)}, u32[]{:S(2)}, u32[]{:S(2)}) async-start(f32[16,1,512]{2,1,0:T(1,128)} %reshape.69), calls=%async_computation | async-start | bytes 65536 | tf_op jit(solution)/shard_map/all_to_all | solution.py:51
  17.8 4.4 %convolution_convert_fusion = bf16[16,64,2048]{2,1,0:T(8,128)(2,1)} fusion(bf16[256,2048]{1,0:T(8,128)(2,1)} %param.6, s32[16,256]{1,0:T(8,128)S(1)} %copy_bitcast_fusion.1, pred[16,256]{1,0:T(8,128)(4,1)S(1)} %bitcast.63), kind=kOutput, calls=%fused_computation.13 | convolution fusion | flops 1076363264 | bytes 5263360 | tf_op jit(solution)/shard_map/qct,td->qcd/dot_general | solution.py:49
  22.2 2.7 all-to-all-done
  24.9 4.8 %all-to-all-start.1 = ((bf16[16,64,2048]{2,1,0:T(8,128)(2,1)}), bf16[16,64,2048]{2,1,0:T(8,128)(2,1)}, u32[]{:S(2)}, u32[]{:S(2)}) async-start(bf16[16,64,2048]{2,1,0:T(8,128)(2,1)} %convolution_convert_fusion), calls=%async_computation.1 | async-start | bytes 8388608 | tf_op jit(solution)/shard_map/all_to_all | solution.py:50
  29.8 0.5 broadcast.66
  30.3 0.7 reduce.4
  31.2 2.3 reduce-window.16
  33.5 0.3 slice_reduce_fusion
  34.0 88.9 %all-to-all-done.1 = bf16[16,64,2048]{2,1,0:T(8,128)(2,1)} async-done(((bf16[16,64,2048]{2,1,0:T(8,128)(2,1)}), bf16[16,64,2048]{2,1,0:T(8,128)(2,1)}, u32[]{:S(2)}, u32[]{:S(2)}) %all-to-all-start.1) | async-done | bytes 4194336 | tf_op jit(solution)/shard_map/all_to_all | solution.py:50
  122.9 13.9 %fusion.7 = bf16[8,256,2048]{2,1,0:T(8,128)(2,1)} fusion(bf16[1024,2048,1]{1,0,2:T(8,128)(2,1)} %bitcast.8, s32[8,1024]{1,0:T(8,128)S(1)} %bitcast.65, pred[8,1024]{1,0:T(8,128)(4,1)S(1)} %get-tuple-element.6), kind=kOutput, calls=%fused_computation.8 | convolution fusion | flops 8598323200 | bytes 12623872 | tf_op jit(solution)/shard_map/lcr,rd->lcd/dot_general | solution.py:18
  136.8 18.1 %fusion.28 = f32[8,256,768]{2,1,0:T(8,128)} fusion(bf16[8,256,2048]{2,1,0:T(8,128)(2,1)} %fusion.7, bf16[8,2048,768]{2,1,0:T(8,128)(2,1)} %param.10), kind=kOutput, calls=%fused_computation.44 | convolution fusion | flops 6442450944 | bytes 39845888 | tf_op jit(solution)/shard_map/lcd,ldf->lcf/dot_general | solution.py:9
  154.9 18.1 %fusion.27 = f32[8,256,768]{2,1,0:T(8,128)} fusion(bf16[8,256,2048]{2,1,0:T(8,128)(2,1)} %fusion.7, bf16[8,2048,768]{2,1,0:T(8,128)(2,1)} %param.9), kind=kOutput, calls=%fused_computation.43 | convolution fusion | flops 6442450944 | bytes 39845888 | tf_op jit(solution)/shard_map/lcd,ldf->lcf/dot_general | solution.py:8
  173.0 19.7 %fusion.46 = bf16[8,256,2048]{2,1,0:T(8,128)(2,1)} fusion(bf16[8,768,2048]{2,1,0:T(8,128)(2,1)} %param.11, f32[8,256,768]{2,1,0:T(8,128)} %fusion.28, f32[8,256,768]{2,1,0:T(8,128)} %fusion.27), kind=kOutput, calls=%fused_computation.1.clone.2 | convolution fusion | flops 6456082432 | bytes 46137344 | tf_op jit(solution)/shard_map/lcf,lfd->lcd/dot_general | solution.py:11
  192.7 14.3 %multiply_reduce_fusion = bf16[1024,2048]{1,0:T(8,128)(2,1)S(1)} fusion(f32[8,1024]{1,0:T(8,128)S(1)} %bitcast.61, s32[8,1024]{1,0:T(8,128)S(1)} %bitcast.66, pred[8,1024]{1,0:T(8,128)(4,1)S(1)} %get-tuple-element.6, bf16[8,256,2048]{2,1,0:T(8,128)(2,1)} %fusion.46), kind=kOutput, calls=%fused_computation | convolution fusion | flops 8625586176 | bytes 12656640 | tf_op jit(solution)/shard_map/lcr,lcd->lrd/dot_general | solution.py:20
  207.0 103.5 %all_to_all.15 = bf16[16,64,2048]{2,1,0:T(8,128)(2,1)S(1)} all-to-all(bf16[16,64,2048]{2,1,0:T(8,128)(2,1)S(1)} %bitcast.57), channel_id=1, replica_groups=mesh['dp'=4,'ep'=16] {'ep'}, dimensions={0} | all-to-all | bytes 8388608 | tf_op jit(solution)/shard_map/all_to_all | solution.py:53
  310.5 2.3 fusion.17
  (18 shorter events, 1.0 us)
Async XLA Ops:
  7.1 17.9 %all-to-all-start = ((f32[16,1,512]{2,1,0:T(1,128)}), f32[16,1,512]{2,1,0:T(1,128)S(1)}, u32[]{:S(2)}, u32[]{:S(2)}) async-start(f32[16,1,512]{2,1,0:T(1,128)} %reshape.69), calls=%async_computation | async-start | bytes 65536 | tf_op jit(solution)/shard_map/all_to_all | solution.py:51
  24.9 98.0 %all-to-all-start.1 = ((bf16[16,64,2048]{2,1,0:T(8,128)(2,1)}), bf16[16,64,2048]{2,1,0:T(8,128)(2,1)}, u32[]{:S(2)}, u32[]{:S(2)}) async-start(bf16[16,64,2048]{2,1,0:T(8,128)(2,1)} %convolution_convert_fusion), calls=%async_computation.1 | async-start | bytes 8388608 | tf_op jit(solution)/shard_map/all_to_all | solution.py:50
  207.0 103.5 %copy-start = (bf16[256,2048]{1,0:T(8,128)(2,1)S(1)}, bf16[256,2048]{1,0:T(8,128)(2,1)}, u32[]{:S(2)}) copy-start(bf16[256,2048]{1,0:T(8,128)(2,1)} %param.6) | copy-start | bytes 3145732
where the time goes:
time: 313 us
  blocking collectives  103 us (33%)
  waiting for transfers between devices  91.6 us (29%)
  matrix products  90.8 us (29%)
  starting transfers between devices  15.6 us (5%)
  other arithmetic  7.41 us (2%)
  local copies, waits for them, and re-layouts  3.83 us (1%)
    all_to_all x1, blocking collectives, device_step(): lax.all_to_all(dev_sum.reshape(groups, pair_cap, d_model), 'ep', 0, 0, ti...  103 us
    all_to_all x1, waiting for transfers between devices, device_step(): recv_rows = lax.all_to_all(send_rows, 'ep', 0, 0, tiled=True)  88.9 us
    dot_general x1, matrix products, expert_ffn(): jnp.einsum('lcf,lfd->lcd', hidden, w_down, preferred_element_type=jnp.flo...  19.7 us
    dot_general x1, matrix products, expert_ffn(): jnp.einsum('lcd,ldf->lcf', expert_in, w_gate, preferred_element_type=jnp....  18.1 us
    dot_general x1, matrix products, expert_ffn(): jnp.einsum('lcd,ldf->lcf', expert_in, w_up, preferred_element_type=jnp.fl...  18.1 us
    dot_general x1, matrix products, serve_rows(): jnp.einsum('lcr,lcd->lrd', fan_mat, expert_out, preferred_element_type=jn...  14.3 us
    dot_general x1, matrix products, serve_rows(): jnp.einsum('lcr,rd->lcd', fan_mat, recv_rows, preferred_element_type=jnp....  13.9 us
    all_to_all x1, starting transfers between devices, device_step(): recv_gate = lax.all_to_all(send_gate, 'ep', 0, 0, tiled=True)  10.7 us
  transfers between devices with their start and end apart: 2, of which 2 were waited for; matrix products, arithmetic and copies ran while one was open for 3% of the time, Pallas kernels for 0%

commit v1 on v0

v1 whole, which is shorter than its diff:
```python
import functools

import jax
import jax.numpy as jnp
from jax import lax
from jax.experimental import pallas as pl
from jax.experimental.pallas import tpu as pltpu
from jax.sharding import PartitionSpec as P

MESH = pl.DeviceIdType.MESH
SUBS = 4
F32 = jnp.float32
BF16 = jnp.bfloat16


def dot(a, b):
    return jnp.dot(a, b, preferred_element_type=F32)


def dot_nt(a, b, precision=None):
    return lax.dot_general(a, b, (((1,), (1,)), ((), ())), precision=precision, preferred_element_type=F32)


def dot_tn(a, b):
    return lax.dot_general(a, b, (((0,), (0,)), ((), ())), preferred_element_type=F32)


def moe_kernel(groups, tok, meta_in, w_gate, w_up, w_down, out, xall, meta, rows, acc, ret, wgb, wub, wdb, xin, hid, fan, fan_t,
               slot_r, slot_c, gate_c, comb, tri, base_r, base_c, ring_s, ring_r, sib_s, sib_r, mring_s, mring_r, msib_s, msib_r,
               ret_s, ret_r, wsem, loc):
    nz = groups // 2
    half = nz // 2
    tok_dev, d_model = tok.shape
    local, _, ffn = w_gate.shape
    top_k = meta.shape[1] // 2
    cap = tok_dev * (top_k // 2) // groups
    ecap = fan.shape[0]
    sub_rows = tok_dev // SUBS
    blk = 2 * cap
    nt = min(512, d_model)
    ft = min(256, ffn)
    far = nz - 1
    split = 2 * half - 3

    me = lax.axis_index('ep')
    z = me // 2
    k = me % 2
    right = ((z + 1) % nz) * 2 + k
    left = ((z + nz - 1) % nz) * 2 + k
    sib = z * 2 + 1 - k

    def source_shift(j):
        if j == 0:
            return 0
        if j == far:
            return half
        return nz - (j + 1) // 2 if j % 2 == 1 else j // 2

    def device_at(shift, c):
        return ((z + shift) % nz) * 2 + (k if c == 0 else 1 - k)

    def remote(src, dst, ssem, rsem, dev):
        return pltpu.make_async_remote_copy(src_ref=src, dst_ref=dst, send_sem=ssem, recv_sem=rsem, device_id={'ep': dev}, device_id_type=MESH)

    def sub_ds(sub, c=0):
        return pl.ds(c * tok_dev + sub * sub_rows, sub_rows)

    def ring_copy(src, dst_j, sub, dev):
        return remote(src, xall.at[dst_j, sub_ds(sub)], ring_s.at[dst_j, sub], ring_r.at[dst_j, sub], dev)

    def sib_copy(src, j, sub):
        return remote(src, xall.at[j, sub_ds(sub, 1)], sib_s.at[j, sub], sib_r.at[j, sub], sib)

    def mring_copy(src, dst_j, dev):
        return remote(src, meta.at[dst_j, :, pl.ds(0, tok_dev)], mring_s.at[dst_j], mring_r.at[dst_j], dev)

    def msib_copy(src, j):
        return remote(src, meta.at[j, :, pl.ds(tok_dev, tok_dev)], msib_s.at[j], msib_r.at[j], sib)

    def ret_copy(j, c):
        off = j * blk + c * cap
        return remote(rows.at[pl.ds(off, cap)], ret.at[pl.ds(off, cap)], ret_s.at[j, c], ret_r.at[j, c], device_at(source_shift(j), c))

    def weight_copies(expert, slot):
        return (pltpu.make_async_copy(w_gate.at[expert], wgb.at[slot], wsem.at[slot, 0]),
                pltpu.make_async_copy(w_up.at[expert], wub.at[slot], wsem.at[slot, 1]),
                pltpu.make_async_copy(w_down.at[expert], wdb.at[slot], wsem.at[slot, 2]))

    own_tok = pltpu.make_async_copy(tok, xall.at[0, pl.ds(0, tok_dev)], loc.at[0])
    own_meta = pltpu.make_async_copy(meta_in, meta.at[0, :, pl.ds(0, tok_dev)], loc.at[1])
    own_meta.start()
    own_tok.start()

    barrier = pltpu.get_barrier_semaphore()
    for step in range(1, groups):
        pl.semaphore_signal(barrier, inc=1, device_id={'ep': (me + step) % groups}, device_id_type=MESH)
    pl.semaphore_wait(barrier, groups - 1)

    mring_copy(meta_in, 1, right).start()
    mring_copy(meta_in, 2, left).start()
    msib_copy(meta_in, 0).start()
    for sub in range(SUBS):
        ring_copy(tok.at[sub_ds(sub)], 1, sub, right).start()
        ring_copy(tok.at[sub_ds(sub)], 2, sub, left).start()
    for sub in range(SUBS):
        sib_copy(tok.at[sub_ds(sub)], 0, sub).start()
    for copy in weight_copies(0, 0):
        copy.start()

    def relay_meta(j, next_j, dev):
        mring_copy(meta_in, j, dev).wait_recv()
        here = meta.at[j, :, pl.ds(0, tok_dev)]
        if next_j is not None:
            mring_copy(here, next_j, dev).start()
        msib_copy(here, j).start()

    def relay_sub(j, sub, next_j, dev):
        here = xall.at[j, sub_ds(sub)]
        ring_copy(here, j, sub, dev).wait_recv()
        if next_j is not None:
            ring_copy(here, next_j, sub, dev).start()
        sib_copy(here, j, sub).start()

    def wait_sib(j):
        msib_copy(meta.at[j, :, pl.ds(0, tok_dev)], j).wait_recv()
        for sub in range(SUBS):
            sib_copy(xall.at[j, sub_ds(sub)], j, sub).wait_recv()

    tok_row = lax.broadcasted_iota(jnp.int32, (tok_dev, tok_dev), 0)
    tok_col = lax.broadcasted_iota(jnp.int32, (tok_dev, tok_dev), 1)
    tri[...] = jnp.where(tok_row < tok_col, 1.0, 0.0).astype(BF16)

    own_meta.wait()
    row_id = lax.broadcasted_iota(jnp.int32, (2 * nz, tok_dev), 0)
    peer_lo = jnp.zeros((2 * nz, tok_dev), jnp.int32)
    for j in range(nz):
        for c in range(2):
            peer = device_at((nz - source_shift(j)) % nz, c)
            peer_lo = jnp.where(row_id == 2 * j + c, peer * local, peer_lo)
    peer_lo = peer_lo.astype(F32)
    own_ids = meta[0, 0:top_k, 0:tok_dev]
    picked = jnp.zeros((2 * nz, tok_dev), F32)
    for i in range(top_k):
        rel = own_ids[i:i + 1, :] - peer_lo
        picked = jnp.where((rel >= 0) & (rel < local), 1.0, picked)
    rank = jnp.where(picked > 0, dot(picked.astype(BF16), tri[...]), -1.0)
    cap_iota = lax.broadcasted_iota(jnp.int32, (cap, tok_dev), 0).astype(F32)
    for r in range(2 * nz):
        comb[r * cap:(r + 1) * cap, :] = jnp.where(rank[r:r + 1, :] == cap_iota, 1.0, 0.0).astype(BF16)

    lo = (me * local).astype(F32)

    def reset_base():
        base_r[...] = jnp.zeros_like(base_r)
        base_c[...] = jnp.zeros_like(base_c)

    def pack_slot(j, carry):
        ids = meta[j, 0:top_k, :]
        gts = meta[j, top_k:2 * top_k, :]
        rel = ids - lo
        chosen = jnp.max(jnp.where((rel >= 0) & (rel < local), 1.0, 0.0), axis=0, keepdims=True)
        halves = []
        for c in range(2):
            ch = jnp.broadcast_to(chosen[:, c * tok_dev:(c + 1) * tok_dev], (8, tok_dev)).astype(BF16)
            halves.append(dot(ch, tri[...])[0:1, :] + float(c * cap))
        rank2 = jnp.where(chosen > 0, jnp.concatenate(halves, axis=1), -1.0)
        pack = jnp.where(rank2 == lax.broadcasted_iota(jnp.int32, (blk, 2 * tok_dev), 0).astype(F32), 1.0, 0.0)
        pack_b = pack.astype(BF16)
        loc_iota = lax.broadcasted_iota(jnp.int32, (local, 2 * tok_dev), 0).astype(F32)
        mem = jnp.zeros((local, 2 * tok_dev), F32)
        gat = jnp.zeros((local, 2 * tok_dev), F32)
        for i in range(top_k):
            hit = rel[i:i + 1, :] == loc_iota
            mem = jnp.where(hit, 1.0, mem)
            gat = jnp.where(hit, gts[i:i + 1, :], gat)
        mem_b = mem.astype(BF16)
        mem_r = dot_nt(mem_b, pack_b)
        mem_c = dot_nt(pack_b, mem_b)
        gate_j = dot_nt(pack, gat, lax.Precision.HIGHEST)
        tri_b = tri[0:blk, 0:blk]
        pos_r = dot(mem_r.astype(BF16), tri_b) + base_r[...]
        pos_c = dot_tn(tri_b, mem_c.astype(BF16)) + base_c[...]
        here = pl.ds(pl.multiple_of(j * blk, blk), blk)
        slot_r[:, here] = jnp.where(mem_r > 0, pos_r, -1.0)
        slot_c[here, :] = jnp.where(mem_c > 0, pos_c, -1.0)
        gate_c[here, :] = gate_j
        base_r[...] += jnp.sum(mem_r, axis=1, keepdims=True)
        base_c[...] += jnp.sum(mem_c, axis=0, keepdims=True)

        def tile(n, carry):
            cols = pl.ds(pl.multiple_of(n * nt, nt), nt)
            rows[here, cols] = dot(pack_b, xall[j, :, cols]).astype(BF16)
            return carry

        lax.fori_loop(0, d_model // nt, tile, 0)
        return carry

    def expert_pass(j0, j1, last, hook):
        r0, count = j0 * blk, (j1 - j0) * blk

        def zero(i, carry):
            acc[pl.ds(pl.multiple_of(i * blk, blk), blk), :] = jnp.zeros((blk, d_model), F32)
            return carry

        lax.fori_loop(0, j1 - j0, zero, 0)

        def expert(l, carry):
            slot = l % 2
            hook(l)

            def prefetch():
                for copy in weight_copies((l + 1) % local, (l + 1) % 2):
                    copy.start()

            if last:
                pl.when(l < local - 1)(prefetch)
            else:
                prefetch()
            lane = lax.broadcasted_iota(jnp.int32, (count, local), 1) == l
            pos = jnp.sum(jnp.where(lane, slot_c[r0:r0 + count, :], 0.0), axis=1, keepdims=True)
            gate = jnp.sum(jnp.where(lane, gate_c[r0:r0 + count, :], 0.0), axis=1, keepdims=True)
            fan_t[0:count, :] = jnp.where(pos == lax.broadcasted_iota(jnp.int32, (count, ecap), 1).astype(F32), 1.0, 0.0).astype(BF16)
            row_pos = slot_r[pl.ds(l, 1), r0:r0 + count]
            fan[:, 0:count] = jnp.where(row_pos == lax.broadcasted_iota(jnp.int32, (ecap, count), 0).astype(F32), 1.0, 0.0).astype(BF16)

            def gather(n, carry):
                cols = pl.ds(pl.multiple_of(n * nt, nt), nt)
                xin[:, cols] = dot(fan[:, 0:count], rows[r0:r0 + count, cols]).astype(BF16)
                return carry

            lax.fori_loop(0, d_model // nt, gather, 0)
            copies = weight_copies(l, slot)
            copies[0].wait()
            copies[1].wait()

            def inner(f, carry):
                cols = pl.ds(pl.multiple_of(f * ft, ft), ft)
                gate_act = dot(xin[...], wgb[slot, :, cols])
                up_act = dot(xin[...], wub[slot, :, cols])
                hid[:, cols] = (jax.nn.silu(gate_act) * up_act).astype(BF16)
                return carry

            lax.fori_loop(0, ffn // ft, inner, 0)
            copies[2].wait()

            def down(n, carry):
                cols = pl.ds(pl.multiple_of(n * nt, nt), nt)
                y = dot(hid[...], wdb[slot, :, cols]).astype(BF16)
                acc[0:count, cols] += gate * dot(fan_t[0:count, :], y)
                return carry

            lax.fori_loop(0, d_model // nt, down, 0)
            return carry

        lax.fori_loop(0, local, expert, 0)

        def finish(i, carry):
            rows[pl.ds(pl.multiple_of(r0 + i * blk, blk), blk), :] = acc[pl.ds(pl.multiple_of(i * blk, blk), blk), :].astype(BF16)
            return carry

        lax.fori_loop(0, j1 - j0, finish, 0)

    reset_base()
    own_tok.wait()
    wait_sib(0)
    lax.fori_loop(0, 1, pack_slot, 0)
    for s in range(1, half - 1):
        jr, jl = 2 * s - 1, 2 * s
        relay_meta(jr, jr + 2, right)
        relay_meta(jl, jl + 2, left)
        for sub in range(SUBS):
            relay_sub(jr, sub, jr + 2, right)
            relay_sub(jl, sub, jl + 2, left)
        wait_sib(jr)
        wait_sib(jl)
        lax.fori_loop(jr, jl + 1, pack_slot, 0)

    jr, jl = split, split + 1

    def hook_a(l):
        def meta_step():
            relay_meta(jr, far, right)
            relay_meta(jl, None, left)

        def data_step():
            sub = l - 2
            for j, dev, toward in ((jr, right, sub < SUBS // 2), (jl, left, sub >= SUBS // 2)):
                here = xall.at[j, sub_ds(sub)]
                ring_copy(here, j, sub, dev).wait_recv()

                def forward():
                    ring_copy(here, far, sub, dev).start()

                pl.when(toward)(forward)
                sib_copy(here, j, sub).start()

        pl.when(l == 1)(meta_step)
        pl.when((l >= 2) & (l < 2 + SUBS))(data_step)

    expert_pass(0, split, False, hook_a)
    ret[0:cap, :] = rows[0:cap, :]
    for j in list(range(split - 1, -1, -1)):
        for c in range(2):
            if (j, c) != (0, 0):
                ret_copy(j, c).start()

    relay_meta(far, None, right)
    for sub in range(SUBS):
        relay_sub(far, sub, None, right)
    reset_base()
    for j in (jr, jl, far):
        wait_sib(j)
    lax.fori_loop(split, nz, pack_slot, 0)
    expert_pass(split, nz, True, lambda l: None)
    for j in range(nz - 1, split - 1, -1):
        for c in range(2):
            ret_copy(j, c).start()

    near = split * blk
    for j in range(split):
        for c in range(2):
            if (j, c) != (0, 0):
                ret_copy(j, c).wait_recv()

    def first(n, carry):
        cols = pl.ds(pl.multiple_of(n * nt, nt), nt)
        acc[0:tok_dev, cols] = xall[0, 0:tok_dev, cols].astype(F32) + dot_tn(comb[0:near, :], ret[0:near, cols])
        return carry

    lax.fori_loop(0, d_model // nt, first, 0)
    for j in range(split, nz):
        for c in range(2):
            ret_copy(j, c).wait_recv()

    def second(n, carry):
        cols = pl.ds(pl.multiple_of(n * nt, nt), nt)
        out[:, cols] = (acc[0:tok_dev, cols] + dot_tn(comb[near:, :], ret[near:, cols])).astype(BF16)
        return carry

    lax.fori_loop(0, d_model // nt, second, 0)

    for j in range(nz):
        msib_copy(meta_in, j).wait_send()
        if j > 0:
            mring_copy(meta_in, j, right).wait_send()
        for sub in range(SUBS):
            sib_copy(tok.at[sub_ds(sub)], j, sub).wait_send()
            if j > 0:
                ring_copy(tok.at[sub_ds(sub)], j, sub, right).wait_send()
        for c in range(2):
            if (j, c) != (0, 0):
                ret_copy(j, c).wait_send()


def solution(mesh):
    groups = mesh.shape['ep']
    nz = groups // 2
    row_spec = P(('dp', 'ep'))
    expert_spec = P('ep')

    def device_step(tokens, expert_ids, gate_vals, w_gate, w_up, w_down):
        tok_dev, top_k = expert_ids.shape
        d_model = tokens.shape[1]
        local, _, ffn = w_gate.shape
        cap = tok_dev * (top_k // 2) // groups
        ecap = tok_dev * top_k // local
        row_count = groups * cap
        near = (2 * (nz // 2) - 3) * 2 * cap
        meta = jnp.concatenate([expert_ids.T.astype(F32), gate_vals.T], axis=0)
        hbm = pl.BlockSpec(memory_space=pl.ANY)
        dma = pltpu.SemaphoreType.DMA
        return pl.pallas_call(
            functools.partial(moe_kernel, groups),
            out_shape=jax.ShapeDtypeStruct(tokens.shape, tokens.dtype),
            in_specs=[hbm] * 5,
            out_specs=pl.BlockSpec(memory_space=pltpu.VMEM),
            scratch_shapes=[
                pltpu.VMEM((nz, 2 * tok_dev, d_model), BF16),
                pltpu.VMEM((nz, 2 * top_k, 2 * tok_dev), F32),
                pltpu.VMEM((row_count, d_model), BF16),
                pltpu.VMEM((near, d_model), F32),
                pltpu.VMEM((row_count, d_model), BF16),
                pltpu.VMEM((2, d_model, ffn), BF16),
                pltpu.VMEM((2, d_model, ffn), BF16),
                pltpu.VMEM((2, ffn, d_model), BF16),
                pltpu.VMEM((ecap, d_model), BF16),
                pltpu.VMEM((ecap, ffn), BF16),
                pltpu.VMEM((ecap, near), BF16),
                pltpu.VMEM((near, ecap), BF16),
                pltpu.VMEM((local, row_count), F32),
                pltpu.VMEM((row_count, local), F32),
                pltpu.VMEM((row_count, local), F32),
                pltpu.VMEM((row_count, tok_dev), BF16),
                pltpu.VMEM((tok_dev, tok_dev), BF16),
                pltpu.VMEM((local, 1), F32),
                pltpu.VMEM((1, local), F32),
                dma((nz, SUBS)), dma((nz, SUBS)), dma((nz, SUBS)), dma((nz, SUBS)),
                dma((nz,)), dma((nz,)), dma((nz,)), dma((nz,)),
                dma((nz, 2)), dma((nz, 2)), dma((2, 3)), dma((2,)),
            ],
            compiler_params=pltpu.CompilerParams(collective_id=0, has_side_effects=True, vmem_limit_bytes=67043328),
            name='moe_fused',
        )(tokens, meta, w_gate, w_up, w_down)

    return jax.shard_map(device_step, mesh=mesh, in_specs=(row_spec, row_spec, row_spec, expert_spec, expert_spec, expert_spec), out_specs=row_spec, check_vma=False)
```

time: 313 us -> 241 us (0.77)
  Pallas kernels: 0 us -> 236 us
  blocking collectives: 103 us -> 0 us
  waiting for transfers between devices: 91.6 us -> 0 us
  matrix products: 90.8 us -> 0 us
  starting transfers between devices: 15.6 us -> 0 us
  other arithmetic: 7.41 us -> 2 us
    pallas_call x0 -> x1, Pallas kernels: none -> 236 us  [device_step(): pl.pallas_call(functools.partial(moe_kernel, groups), out_shape=jax.Shape...]
    all_to_all x1 -> x0, blocking collectives: 103 us -> none  [device_step(): lax.all_to_all(dev_sum.reshape(groups, pair_cap, d_model), 'ep', 0, 0, ti...]
    all_to_all x2 -> x0, waiting for transfers between devices: 91.6 us -> none  [the longest x1 88.9 us: device_step(): recv_rows = lax.all_to_all(send_rows, 'ep', 0, 0, tiled=True)]
    dot_general x7 -> x0, matrix products: 90.8 us -> none  [the longest x1 19.7 us: expert_ffn(): jnp.einsum('lcf,lfd->lcd', hidden, w_down, preferred_element_type=jnp.flo...]
    all_to_all x2 -> x0, starting transfers between devices: 15.6 us -> none  [the longest x1 10.7 us: device_step(): recv_gate = lax.all_to_all(send_gate, 'ep', 0, 0, tiled=True)]
  transfers between devices with their start and end apart: 2 -> 0, of which waited for: 2 -> 0; matrix products, arithmetic and copies ran while one was open for 3% -> 0% of each run, Pallas kernels for 0% -> 0%
where the time goes in v1:
time: 241 us
  Pallas kernels  236 us (98%)
    pallas_call x1, Pallas kernels, device_step(): pl.pallas_call(functools.partial(moe_kernel, groups), out_shape=jax.Shape...  236 us

profile of v1, /device:TPU:21, one launch (start us, length us, event | category | flops | bytes accessed | tf_op | source)
XLA Modules:
  0.0 240.6 jit_solution(5073928928532389476)
XLA Ops:
  0.0 0.7 convert_bitcast_fusion
  0.7 1.3 pad_maximum_fusion.meta_in
  2.0 236.3 %moe_fused.1 = bf16[256,2048]{1,0:T(8,128)(2,1)} custom-call(bf16[256,2048]{1,0:T(8,128)(2,1)} %tok.1, f32[16,256]{1,0:T(8,128)} %pad_maximum_fusion.meta_in, bf16[8,2048,768]{2,1,0:T(8,128)(2,1)} %w_gate.1, bf16[8,2048,768]{2,1,0:T(8,128)(2,1)} %w_up.1, bf16[8,768,2048]{2,1,0:T(8,128)(2,1)} %w_down.1), custom_call_target="tpu_custom_call" | custom-call | tf_op jit(solution)/shard_map/moe_fused/pallas_call | solution.py:372
  238.3 2.3 copy.8

commit v2 on v1

--- a/solution.py
+++ b/solution.py
@@ -223,33 +223,17 @@
             row_pos = slot_r[pl.ds(l, 1), r0:r0 + count]
             fan[:, 0:count] = jnp.where(row_pos == lax.broadcasted_iota(jnp.int32, (ecap, count), 0).astype(F32), 1.0, 0.0).astype(BF16)
 
-            def gather(n, carry):
-                cols = pl.ds(pl.multiple_of(n * nt, nt), nt)
-                xin[:, cols] = dot(fan[:, 0:count], rows[r0:r0 + count, cols]).astype(BF16)
-                return carry
-
-            lax.fori_loop(0, d_model // nt, gather, 0)
-            copies = weight_copies(l, slot)
-            copies[0].wait()
-            copies[1].wait()
-
-            def inner(f, carry):
-                cols = pl.ds(pl.multiple_of(f * ft, ft), ft)
-                gate_act = dot(xin[...], wgb[slot, :, cols])
-                up_act = dot(xin[...], wub[slot, :, cols])
-                hid[:, cols] = (jax.nn.silu(gate_act) * up_act).astype(BF16)
-                return carry
-
-            lax.fori_loop(0, ffn // ft, inner, 0)
-            copies[2].wait()
-
-            def down(n, carry):
-                cols = pl.ds(pl.multiple_of(n * nt, nt), nt)
-                y = dot(hid[...], wdb[slot, :, cols]).astype(BF16)
-                acc[0:count, cols] += gate * dot(fan_t[0:count, :], y)
-                return carry
-
-            lax.fori_loop(0, d_model // nt, down, 0)
+            for copy in weight_copies(l, slot):
+                copy.wait()
+            for n in range(0, d_model, nt):
+                xin[:, n:n + nt] = dot(fan[:, 0:count], rows[r0:r0 + count, n:n + nt]).astype(BF16)
+            for f in range(0, ffn, ft):
+                gate_act = dot(xin[...], wgb[slot, :, f:f + ft])
+                up_act = dot(xin[...], wub[slot, :, f:f + ft])
+                hid[:, f:f + ft] = (jax.nn.silu(gate_act) * up_act).astype(BF16)
+            for n in range(0, d_model, nt):
+                y = dot(hid[...], wdb[slot, :, n:n + nt]).astype(BF16)
+                acc[0:count, n:n + nt] += gate * dot(fan_t[0:count, :], y)
             return carry
 
         lax.fori_loop(0, local, expert, 0)

time: 241 us -> 213 us (0.88)
  Pallas kernels: 236 us -> 209 us
    pallas_call x1, Pallas kernels: 236 us -> 209 us  [device_step(): pl.pallas_call(functools.partial(moe_kernel, groups), out_shape=jax.Shape...]
where the time goes in v2:
time: 213 us
  Pallas kernels  209 us (98%)
  local copies, waits for them, and re-layouts  2.3 us (1%)
    pallas_call x1, Pallas kernels, device_step(): pl.pallas_call(functools.partial(moe_kernel, groups), out_shape=jax.Shape...  209 us

profile of v2, /device:TPU:21, one launch (start us, length us, event | category | flops | bytes accessed | tf_op | source)
XLA Modules:
  0.0 213.0 jit_solution(16983170534578432572)
XLA Ops:
  0.0 0.7 convert_bitcast_fusion
  0.7 1.3 pad_maximum_fusion.meta_in
  2.0 208.7 %moe_fused.1 = bf16[256,2048]{1,0:T(8,128)(2,1)} custom-call(bf16[256,2048]{1,0:T(8,128)(2,1)} %tok.1, f32[16,256]{1,0:T(8,128)} %pad_maximum_fusion.meta_in, bf16[8,2048,768]{2,1,0:T(8,128)(2,1)} %w_gate.1, bf16[8,2048,768]{2,1,0:T(8,128)(2,1)} %w_up.1, bf16[8,768,2048]{2,1,0:T(8,128)(2,1)} %w_down.1), custom_call_target="tpu_custom_call" | custom-call | tf_op jit(solution)/shard_map/moe_fused/pallas_call | solution.py:356
  210.7 2.3 %copy.8 = bf16[256,2048]{1,0:T(8,128)(2,1)} copy(bf16[256,2048]{1,0:T(8,128)(2,1)} %moe_fused.1) | data formatting | bytes 2097152

commit v3 on v2

--- a/solution.py
+++ b/solution.py
@@ -25,14 +25,14 @@
     return lax.dot_general(a, b, (((0,), (0,)), ((), ())), preferred_element_type=F32)
 
 
-def moe_kernel(groups, tok, meta_in, w_gate, w_up, w_down, out, xall, meta, rows, acc, ret, wgb, wub, wdb, xin, hid, fan, fan_t,
+def moe_kernel(groups, tok, ids_in, gates_in, w_gate, w_up, w_down, out, xall, ids_all, gates_all, rows, acc, ret, wgb, wub, wdb, xin, hid, fan, fan_t,
                slot_r, slot_c, gate_c, comb, tri, base_r, base_c, ring_s, ring_r, sib_s, sib_r, mring_s, mring_r, msib_s, msib_r,
                ret_s, ret_r, wsem, loc):
     nz = groups // 2
     half = nz // 2
     tok_dev, d_model = tok.shape
     local, _, ffn = w_gate.shape
-    top_k = meta.shape[1] // 2
+    top_k = ids_in.shape[0]
     cap = tok_dev * (top_k // 2) // groups
     ecap = fan.shape[0]
     sub_rows = tok_dev // SUBS
@@ -71,11 +71,16 @@
     def sib_copy(src, j, sub):
         return remote(src, xall.at[j, sub_ds(sub, 1)], sib_s.at[j, sub], sib_r.at[j, sub], sib)
 
-    def mring_copy(src, dst_j, dev):
-        return remote(src, meta.at[dst_j, :, pl.ds(0, tok_dev)], mring_s.at[dst_j], mring_r.at[dst_j], dev)
-
-    def msib_copy(src, j):
-        return remote(src, meta.at[j, :, pl.ds(tok_dev, tok_dev)], msib_s.at[j], msib_r.at[j], sib)
+    tables = ((ids_in, ids_all), (gates_in, gates_all))
+
+    def table_src(i, j, own):
+        return tables[i][0] if own else tables[i][1].at[j, :, pl.ds(0, tok_dev)]
+
+    def mring_copy(i, src_j, dst_j, dev):
+        return remote(table_src(i, src_j, src_j == 0), tables[i][1].at[dst_j, :, pl.ds(0, tok_dev)], mring_s.at[dst_j, i], mring_r.at[dst_j, i], dev)
+
+    def msib_copy(i, j):
+        return remote(table_src(i, j, j == 0), tables[i][1].at[j, :, pl.ds(tok_dev, tok_dev)], msib_s.at[j, i], msib_r.at[j, i], sib)
 
     def ret_copy(j, c):
         off = j * blk + c * cap
@@ -87,8 +92,9 @@
                 pltpu.make_async_copy(w_down.at[expert], wdb.at[slot], wsem.at[slot, 2]))
 
     own_tok = pltpu.make_async_copy(tok, xall.at[0, pl.ds(0, tok_dev)], loc.at[0])
-    own_meta = pltpu.make_async_copy(meta_in, meta.at[0, :, pl.ds(0, tok_dev)], loc.at[1])
-    own_meta.start()
+    own_tables = [pltpu.make_async_copy(tables[i][0], tables[i][1].at[0, :, pl.ds(0, tok_dev)], loc.at[1 + i]) for i in range(2)]
+    for copy in own_tables:
+        copy.start()
     own_tok.start()
 
     barrier = pltpu.get_barrier_semaphore()
@@ -96,9 +102,10 @@
         pl.semaphore_signal(barrier, inc=1, device_id={'ep': (me + step) % groups}, device_id_type=MESH)
     pl.semaphore_wait(barrier, groups - 1)
 
-    mring_copy(meta_in, 1, right).start()
-    mring_copy(meta_in, 2, left).start()
-    msib_copy(meta_in, 0).start()
+    for i in range(2):
+        mring_copy(i, 0, 1, right).start()
+        mring_copy(i, 0, 2, left).start()
+        msib_copy(i, 0).start()
     for sub in range(SUBS):
         ring_copy(tok.at[sub_ds(sub)], 1, sub, right).start()
         ring_copy(tok.at[sub_ds(sub)], 2, sub, left).start()
@@ -108,11 +115,11 @@
         copy.start()
 
     def relay_meta(j, next_j, dev):
-        mring_copy(meta_in, j, dev).wait_recv()
-        here = meta.at[j, :, pl.ds(0, tok_dev)]
-        if next_j is not None:
-            mring_copy(here, next_j, dev).start()
-        msib_copy(here, j).start()
+        for i in range(2):
+            mring_copy(i, j, j, dev).wait_recv()
+            if next_j is not None:
+                mring_copy(i, j, next_j, dev).start()
+            msib_copy(i, j).start()
 
     def relay_sub(j, sub, next_j, dev):
         here = xall.at[j, sub_ds(sub)]
@@ -122,7 +129,8 @@
         sib_copy(here, j, sub).start()
 
     def wait_sib(j):
-        msib_copy(meta.at[j, :, pl.ds(0, tok_dev)], j).wait_recv()
+        for i in range(2):
+            msib_copy(i, j).wait_recv()
         for sub in range(SUBS):
             sib_copy(xall.at[j, sub_ds(sub)], j, sub).wait_recv()
 
@@ -130,15 +138,15 @@
     tok_col = lax.broadcasted_iota(jnp.int32, (tok_dev, tok_dev), 1)
     tri[...] = jnp.where(tok_row < tok_col, 1.0, 0.0).astype(BF16)
 
-    own_meta.wait()
+    for copy in own_tables:
+        copy.wait()
     row_id = lax.broadcasted_iota(jnp.int32, (2 * nz, tok_dev), 0)
     peer_lo = jnp.zeros((2 * nz, tok_dev), jnp.int32)
     for j in range(nz):
         for c in range(2):
             peer = device_at((nz - source_shift(j)) % nz, c)
             peer_lo = jnp.where(row_id == 2 * j + c, peer * local, peer_lo)
-    peer_lo = peer_lo.astype(F32)
-    own_ids = meta[0, 0:top_k, 0:tok_dev]
+    own_ids = ids_all[0, :, 0:tok_dev]
     picked = jnp.zeros((2 * nz, tok_dev), F32)
     for i in range(top_k):
         rel = own_ids[i:i + 1, :] - peer_lo
@@ -148,16 +156,15 @@
     for r in range(2 * nz):
         comb[r * cap:(r + 1) * cap, :] = jnp.where(rank[r:r + 1, :] == cap_iota, 1.0, 0.0).astype(BF16)
 
-    lo = (me * local).astype(F32)
+    lo = me * local
 
     def reset_base():
         base_r[...] = jnp.zeros_like(base_r)
         base_c[...] = jnp.zeros_like(base_c)
 
     def pack_slot(j, carry):
-        ids = meta[j, 0:top_k, :]
-        gts = meta[j, top_k:2 * top_k, :]
-        rel = ids - lo
+        gts = gates_all[j]
+        rel = ids_all[j] - lo
         chosen = jnp.max(jnp.where((rel >= 0) & (rel < local), 1.0, 0.0), axis=0, keepdims=True)
         halves = []
         for c in range(2):
@@ -166,7 +173,7 @@
         rank2 = jnp.where(chosen > 0, jnp.concatenate(halves, axis=1), -1.0)
         pack = jnp.where(rank2 == lax.broadcasted_iota(jnp.int32, (blk, 2 * tok_dev), 0).astype(F32), 1.0, 0.0)
         pack_b = pack.astype(BF16)
-        loc_iota = lax.broadcasted_iota(jnp.int32, (local, 2 * tok_dev), 0).astype(F32)
+        loc_iota = lax.broadcasted_iota(jnp.int32, (local, 2 * tok_dev), 0)
         mem = jnp.zeros((local, 2 * tok_dev), F32)
         gat = jnp.zeros((local, 2 * tok_dev), F32)
         for i in range(top_k):
@@ -187,12 +194,8 @@
         base_r[...] += jnp.sum(mem_r, axis=1, keepdims=True)
         base_c[...] += jnp.sum(mem_c, axis=0, keepdims=True)
 
-        def tile(n, carry):
-            cols = pl.ds(pl.multiple_of(n * nt, nt), nt)
-            rows[here, cols] = dot(pack_b, xall[j, :, cols]).astype(BF16)
-            return carry
-
-        lax.fori_loop(0, d_model // nt, tile, 0)
+        for n in range(0, d_model, nt):
+            rows[here, n:n + nt] = dot(pack_b, xall[j, :, n:n + nt]).astype(BF16)
         return carry
 
     def expert_pass(j0, j1, last, hook):
@@ -244,61 +247,78 @@
 
         lax.fori_loop(0, j1 - j0, finish, 0)
 
+    first, second = 3, split
+
+    def send_back(order):
+        for j in order:
+            for c in range(2):
+                if (j, c) != (0, 0):
+                    ret_copy(j, c).start()
+
     reset_base()
     own_tok.wait()
     wait_sib(0)
     lax.fori_loop(0, 1, pack_slot, 0)
-    for s in range(1, half - 1):
-        jr, jl = 2 * s - 1, 2 * s
-        relay_meta(jr, jr + 2, right)
-        relay_meta(jl, jl + 2, left)
-        for sub in range(SUBS):
-            relay_sub(jr, sub, jr + 2, right)
-            relay_sub(jl, sub, jl + 2, left)
-        wait_sib(jr)
-        wait_sib(jl)
-        lax.fori_loop(jr, jl + 1, pack_slot, 0)
-
-    jr, jl = split, split + 1
+    for j, dev in ((1, right), (2, left)):
+        relay_meta(j, j + 2, dev)
+    for sub in range(SUBS):
+        relay_sub(1, sub, 3, right)
+        relay_sub(2, sub, 4, left)
+    wait_sib(1)
+    wait_sib(2)
+    lax.fori_loop(1, first, pack_slot, 0)
 
     def hook_a(l):
         def meta_step():
-            relay_meta(jr, far, right)
-            relay_meta(jl, None, left)
-
-        def data_step():
-            sub = l - 2
-            for j, dev, toward in ((jr, right, sub < SUBS // 2), (jl, left, sub >= SUBS // 2)):
-                here = xall.at[j, sub_ds(sub)]
-                ring_copy(here, j, sub, dev).wait_recv()
-
-                def forward():
-                    ring_copy(here, far, sub, dev).start()
-
-                pl.when(toward)(forward)
-                sib_copy(here, j, sub).start()
+            relay_meta(3, 5, right)
+            relay_meta(4, 6, left)
+
+        def data_step(sub):
+            def step():
+                relay_sub(3, sub, 5, right)
+                relay_sub(4, sub, 6, left)
+            return step
 
         pl.when(l == 1)(meta_step)
-        pl.when((l >= 2) & (l < 2 + SUBS))(data_step)
-
-    expert_pass(0, split, False, hook_a)
+        for sub, at in enumerate((2, 4, 5, 7)):
+            pl.when(l == at)(data_step(sub))
+
+    expert_pass(0, first, False, hook_a)
     ret[0:cap, :] = rows[0:cap, :]
-    for j in list(range(split - 1, -1, -1)):
-        for c in range(2):
-            if (j, c) != (0, 0):
-                ret_copy(j, c).start()
-
+    reset_base()
+    wait_sib(3)
+    wait_sib(4)
+    lax.fori_loop(first, second, pack_slot, 0)
+
+    def hook_b(l):
+        def meta_step():
+            relay_meta(5, far, right)
+            relay_meta(6, None, left)
+
+        def data_step(sub):
+            def step():
+                relay_sub(5, sub, far if sub < SUBS // 2 else None, right)
+                relay_sub(6, sub, far if sub >= SUBS // 2 else None, left)
+            return step
+
+        pl.when(l == 0)(meta_step)
+        for sub, at in enumerate((1, 2, 4, 6)):
+            pl.when(l == at)(data_step(sub))
+        pl.when(l == 5)(lambda: send_back((1, 2, 0)))
+
+    expert_pass(first, second, False, hook_b)
+    send_back((3, 4))
+    reset_base()
+    wait_sib(5)
+    wait_sib(6)
+    lax.fori_loop(second, far, pack_slot, 0)
     relay_meta(far, None, right)
     for sub in range(SUBS):
         relay_sub(far, sub, None, right)
-    reset_base()
-    for j in (jr, jl, far):
-        wait_sib(j)
-    lax.fori_loop(split, nz, pack_slot, 0)
-    expert_pass(split, nz, True, lambda l: None)
-    for j in range(nz - 1, split - 1, -1):
-        for c in range(2):
-            ret_copy(j, c).start()
+    wait_sib(far)
+    lax.fori_loop(far, nz, pack_slot, 0)
+    expert_pass(second, nz, True, lambda l: None)
+    send_back((7, 5, 6))
 
     near = split * blk
     for j in range(split):
@@ -306,27 +326,20 @@
             if (j, c) != (0, 0):
                 ret_copy(j, c).wait_recv()
 
-    def first(n, carry):
-        cols = pl.ds(pl.multiple_of(n * nt, nt), nt)
-        acc[0:tok_dev, cols] = xall[0, 0:tok_dev, cols].astype(F32) + dot_tn(comb[0:near, :], ret[0:near, cols])
-        return carry
-
-    lax.fori_loop(0, d_model // nt, first, 0)
+    for n in range(0, d_model, nt):
+        acc[0:tok_dev, n:n + nt] = xall[0, 0:tok_dev, n:n + nt].astype(F32) + dot_tn(comb[0:near, :], ret[0:near, n:n + nt])
     for j in range(split, nz):
         for c in range(2):
             ret_copy(j, c).wait_recv()
 
-    def second(n, carry):
-        cols = pl.ds(pl.multiple_of(n * nt, nt), nt)
-        out[:, cols] = (acc[0:tok_dev, cols] + dot_tn(comb[near:, :], ret[near:, cols])).astype(BF16)
-        return carry
-
-    lax.fori_loop(0, d_model // nt, second, 0)
+    for n in range(0, d_model, nt):
+        out[:, n:n + nt] = (acc[0:tok_dev, n:n + nt] + dot_tn(comb[near:, :], ret[near:, n:n + nt])).astype(BF16)
 
     for j in range(nz):
-        msib_copy(meta_in, j).wait_send()
-        if j > 0:
-            mring_copy(meta_in, j, right).wait_send()
+        for i in range(2):
+            msib_copy(i, j).wait_send()
+            if j > 0:
+                mring_copy(i, 0, j, right).wait_send()
         for sub in range(SUBS):
             sib_copy(tok.at[sub_ds(sub)], j, sub).wait_send()
             if j > 0:
@@ -349,28 +362,28 @@
         cap = tok_dev * (top_k // 2) // groups
         ecap = tok_dev * top_k // local
         row_count = groups * cap
-        near = (2 * (nz // 2) - 3) * 2 * cap
-        meta = jnp.concatenate([expert_ids.T.astype(F32), gate_vals.T], axis=0)
+        most = 3 * 2 * cap
         hbm = pl.BlockSpec(memory_space=pl.ANY)
         dma = pltpu.SemaphoreType.DMA
         return pl.pallas_call(
             functools.partial(moe_kernel, groups),
             out_shape=jax.ShapeDtypeStruct(tokens.shape, tokens.dtype),
-            in_specs=[hbm] * 5,
+            in_specs=[hbm] * 6,
             out_specs=pl.BlockSpec(memory_space=pltpu.VMEM),
             scratch_shapes=[
                 pltpu.VMEM((nz, 2 * tok_dev, d_model), BF16),
-                pltpu.VMEM((nz, 2 * top_k, 2 * tok_dev), F32),
+                pltpu.VMEM((nz, top_k, 2 * tok_dev), jnp.int32),
+                pltpu.VMEM((nz, top_k, 2 * tok_dev), F32),
                 pltpu.VMEM((row_count, d_model), BF16),
-                pltpu.VMEM((near, d_model), F32),
+                pltpu.VMEM((most, d_model), F32),
                 pltpu.VMEM((row_count, d_model), BF16),
                 pltpu.VMEM((2, d_model, ffn), BF16),
                 pltpu.VMEM((2, d_model, ffn), BF16),
                 pltpu.VMEM((2, ffn, d_model), BF16),
                 pltpu.VMEM((ecap, d_model), BF16),
                 pltpu.VMEM((ecap, ffn), BF16),
-                pltpu.VMEM((ecap, near), BF16),
-                pltpu.VMEM((near, ecap), BF16),
+                pltpu.VMEM((ecap, most), BF16),
+                pltpu.VMEM((most, ecap), BF16),
                 pltpu.VMEM((local, row_count), F32),
                 pltpu.VMEM((row_count, local), F32),
                 pltpu.VMEM((row_count, local), F32),
@@ -379,11 +392,11 @@
                 pltpu.VMEM((local, 1), F32),
                 pltpu.VMEM((1, local), F32),
                 dma((nz, SUBS)), dma((nz, SUBS)), dma((nz, SUBS)), dma((nz, SUBS)),
-                dma((nz,)), dma((nz,)), dma((nz,)), dma((nz,)),
-                dma((nz, 2)), dma((nz, 2)), dma((2, 3)), dma((2,)),
+                dma((nz, 2)), dma((nz, 2)), dma((nz, 2)), dma((nz, 2)),
+                dma((nz, 2)), dma((nz, 2)), dma((2, 3)), dma((3,)),
             ],
             compiler_params=pltpu.CompilerParams(collective_id=0, has_side_effects=True, vmem_limit_bytes=67043328),
             name='moe_fused',
-        )(tokens, meta, w_gate, w_up, w_down)
+        )(tokens, expert_ids.T, gate_vals.T, w_gate, w_up, w_down)
 
     return jax.shard_map(device_step, mesh=mesh, in_specs=(row_spec, row_spec, row_spec, expert_spec, expert_spec, expert_spec), out_specs=row_spec, check_vma=False)

time: 213 us -> 222 us (1.042)
  Pallas kernels: 209 us -> 220 us
    pallas_call x1, Pallas kernels: 209 us -> 220 us  [device_step(): pl.pallas_call(functools.partial(moe_kernel, groups), out_shape=jax.Shape...]
where the time goes in v3:
time: 222 us
  Pallas kernels  220 us (99%)
  local copies, waits for them, and re-layouts  2.3 us (1%)
    pallas_call x1, Pallas kernels, device_step(): pl.pallas_call(functools.partial(moe_kernel, groups), out_shape=jax.Shape...  220 us

profile of v3, /device:TPU:21, one launch (start us, length us, event | category | flops | bytes accessed | tf_op | source)
XLA Modules:
  0.0 221.9 jit_solution(2101557793519778687)
XLA Ops:
  0.0 219.6 %moe_fused.1 = bf16[256,2048]{1,0:T(8,128)(2,1)} custom-call(bf16[256,2048]{1,0:T(8,128)(2,1)} %tok.1, s32[8,256]{1,0:T(8,128)} %bitcast.2, f32[8,256]{1,0:T(8,128)} %bitcast.3, bf16[8,2048,768]{2,1,0:T(8,128)(2,1)} %w_gate.1, bf16[8,2048,768]{2,1,0:T(8,128)(2,1)} %w_up.1, bf16[8,768,2048]{2,1,0:T(8,128)(2,1)} %w_down.1), custom_call_target="tpu_custom_call" | custom-call | tf_op jit(solution)/shard_map/moe_fused/pallas_call | solution.py:368
  219.6 2.3 %copy.8 = bf16[256,2048]{1,0:T(8,128)(2,1)} copy(bf16[256,2048]{1,0:T(8,128)(2,1)} %moe_fused.1) | data formatting | bytes 2097152

commit v4 on v3

--- a/solution.py
+++ b/solution.py
@@ -207,6 +207,12 @@
 
         lax.fori_loop(0, j1 - j0, zero, 0)
 
+        def gather(l):
+            row_pos = slot_r[pl.ds(l, 1), r0:r0 + count]
+            fan[:, 0:count] = jnp.where(row_pos == lax.broadcasted_iota(jnp.int32, (ecap, count), 0).astype(F32), 1.0, 0.0).astype(BF16)
+            for n in range(0, d_model, nt):
+                xin[:, n:n + nt] = dot(fan[:, 0:count], rows[r0:r0 + count, n:n + nt]).astype(BF16)
+
         def expert(l, carry):
             slot = l % 2
             hook(l)
@@ -219,26 +225,31 @@
                 pl.when(l < local - 1)(prefetch)
             else:
                 prefetch()
+            for copy in weight_copies(l, slot):
+                copy.wait()
+            for f in range(0, ffn, ft):
+                gate_act = dot(xin[...], wgb[slot, :, f:f + ft])
+                up_act = dot(xin[...], wub[slot, :, f:f + ft])
+                hid[:, f:f + ft] = (jax.nn.silu(gate_act) * up_act).astype(BF16)
+            gather((l + 1) % local)
             lane = lax.broadcasted_iota(jnp.int32, (count, local), 1) == l
             pos = jnp.sum(jnp.where(lane, slot_c[r0:r0 + count, :], 0.0), axis=1, keepdims=True)
             gate = jnp.sum(jnp.where(lane, gate_c[r0:r0 + count, :], 0.0), axis=1, keepdims=True)
             fan_t[0:count, :] = jnp.where(pos == lax.broadcasted_iota(jnp.int32, (count, ecap), 1).astype(F32), 1.0, 0.0).astype(BF16)
-            row_pos = slot_r[pl.ds(l, 1), r0:r0 + count]
-            fan[:, 0:count] = jnp.where(row_pos == lax.broadcasted_iota(jnp.int32, (ecap, count), 0).astype(F32), 1.0, 0.0).astype(BF16)
-
-            for copy in weight_copies(l, slot):
-                copy.wait()
-            for n in range(0, d_model, nt):
-                xin[:, n:n + nt] = dot(fan[:, 0:count], rows[r0:r0 + count, n:n + nt]).astype(BF16)
-            for f in range(0, ffn, ft):
-                gate_act = dot(xin[...], wgb[slot, :, f:f + ft])
-                up_act = dot(xin[...], wub[slot, :, f:f + ft])
-                hid[:, f:f + ft] = (jax.nn.silu(gate_act) * up_act).astype(BF16)
+
+            def spread(n, y):
+                acc[0:count, n:n + nt] += gate * dot(fan_t[0:count, :], y)
+
+            held = None
             for n in range(0, d_model, nt):
                 y = dot(hid[...], wdb[slot, :, n:n + nt]).astype(BF16)
-                acc[0:count, n:n + nt] += gate * dot(fan_t[0:count, :], y)
+                if held is not None:
+                    spread(*held)
+                held = (n, y)
+            spread(*held)
             return carry
 
+        gather(0)
         lax.fori_loop(0, local, expert, 0)
 
         def finish(i, carry):

time: 222 us -> 212 us (0.955)
  Pallas kernels: 220 us -> 209 us
    pallas_call x1, Pallas kernels: 220 us -> 209 us  [device_step(): pl.pallas_call(functools.partial(moe_kernel, groups), out_shape=jax.Shape...]
where the time goes in v4:
time: 212 us
  Pallas kernels  209 us (99%)
  local copies, waits for them, and re-layouts  2.3 us (1%)
    pallas_call x1, Pallas kernels, device_step(): pl.pallas_call(functools.partial(moe_kernel, groups), out_shape=jax.Shape...  209 us

profile of v4, /device:TPU:21, one launch (start us, length us, event | category | flops | bytes accessed | tf_op | source)
XLA Modules:
  0.0 211.7 jit_solution(2378853211271187562)
XLA Ops:
  0.0 209.4 %moe_fused.1 = bf16[256,2048]{1,0:T(8,128)(2,1)} custom-call(bf16[256,2048]{1,0:T(8,128)(2,1)} %tok.1, s32[8,256]{1,0:T(8,128)} %bitcast.2, f32[8,256]{1,0:T(8,128)} %bitcast.3, bf16[8,2048,768]{2,1,0:T(8,128)(2,1)} %w_gate.1, bf16[8,2048,768]{2,1,0:T(8,128)(2,1)} %w_up.1, bf16[8,768,2048]{2,1,0:T(8,128)(2,1)} %w_down.1), custom_call_target="tpu_custom_call" | custom-call | tf_op jit(solution)/shard_map/moe_fused/pallas_call | solution.py:379
  209.4 2.3 %copy.8 = bf16[256,2048]{1,0:T(8,128)(2,1)} copy(bf16[256,2048]{1,0:T(8,128)(2,1)} %moe_fused.1) | data formatting | bytes 2097152

commit v5 on v4

--- a/solution.py
+++ b/solution.py
@@ -26,7 +26,7 @@
 
 
 def moe_kernel(groups, tok, ids_in, gates_in, w_gate, w_up, w_down, out, xall, ids_all, gates_all, rows, acc, ret, wgb, wub, wdb, xin, hid, fan, fan_t,
-               slot_r, slot_c, gate_c, comb, tri, base_r, base_c, ring_s, ring_r, sib_s, sib_r, mring_s, mring_r, msib_s, msib_r,
+               slot_r, slot_c, gate_c, comb, tri, base_r, base_c, packs, ring_s, ring_r, sib_s, sib_r, mring_s, mring_r, msib_s, msib_r,
                ret_s, ret_r, wsem, loc):
     nz = groups // 2
     half = nz // 2
@@ -65,6 +65,9 @@
     def sub_ds(sub, c=0):
         return pl.ds(c * tok_dev + sub * sub_rows, sub_rows)
 
+    def swing(i):
+        return (i + SUBS // 2) % SUBS
+
     def ring_copy(src, dst_j, sub, dev):
         return remote(src, xall.at[dst_j, sub_ds(sub)], ring_s.at[dst_j, sub], ring_r.at[dst_j, sub], dev)
 
@@ -106,9 +109,9 @@
         mring_copy(i, 0, 1, right).start()
         mring_copy(i, 0, 2, left).start()
         msib_copy(i, 0).start()
-    for sub in range(SUBS):
-        ring_copy(tok.at[sub_ds(sub)], 1, sub, right).start()
-        ring_copy(tok.at[sub_ds(sub)], 2, sub, left).start()
+    for i in range(SUBS):
+        ring_copy(tok.at[sub_ds(i)], 1, i, right).start()
+        ring_copy(tok.at[sub_ds(swing(i))], 2, swing(i), left).start()
     for sub in range(SUBS):
         sib_copy(tok.at[sub_ds(sub)], 0, sub).start()
     for copy in weight_copies(0, 0):
@@ -128,9 +131,11 @@
             ring_copy(here, next_j, sub, dev).start()
         sib_copy(here, j, sub).start()
 
-    def wait_sib(j):
+    def wait_sib_tables(j):
         for i in range(2):
             msib_copy(i, j).wait_recv()
+
+    def wait_sib(j):
         for sub in range(SUBS):
             sib_copy(xall.at[j, sub_ds(sub)], j, sub).wait_recv()
 
@@ -162,7 +167,7 @@
         base_r[...] = jnp.zeros_like(base_r)
         base_c[...] = jnp.zeros_like(base_c)
 
-    def pack_slot(j, carry):
+    def slot_tables(j, carry):
         gts = gates_all[j]
         rel = ids_all[j] - lo
         chosen = jnp.max(jnp.where((rel >= 0) & (rel < local), 1.0, 0.0), axis=0, keepdims=True)
@@ -194,11 +199,27 @@
         base_r[...] += jnp.sum(mem_r, axis=1, keepdims=True)
         base_c[...] += jnp.sum(mem_c, axis=0, keepdims=True)
 
+        packs[j % 3] = pack_b
+        return carry
+
+    def pack_rows(j, carry):
+        here = pl.ds(pl.multiple_of(j * blk, blk), blk)
         for n in range(0, d_model, nt):
-            rows[here, n:n + nt] = dot(pack_b, xall[j, :, n:n + nt]).astype(BF16)
+            rows[here, n:n + nt] = dot(packs[j % 3], xall[j, :, n:n + nt]).astype(BF16)
         return carry
 
-    def expert_pass(j0, j1, last, hook):
+    def gather(l, a, b, add):
+        lo_r, hi_r = a * blk, b * blk
+        wide = hi_r - lo_r
+        row_pos = slot_r[pl.ds(l, 1), lo_r:hi_r]
+        fan[:, 0:wide] = jnp.where(row_pos == lax.broadcasted_iota(jnp.int32, (ecap, wide), 0).astype(F32), 1.0, 0.0).astype(BF16)
+        for n in range(0, d_model, nt):
+            got = dot(fan[:, 0:wide], rows[lo_r:hi_r, n:n + nt])
+            if add:
+                got = got + xin[l, :, n:n + nt].astype(F32)
+            xin[l, :, n:n + nt] = got.astype(BF16)
+
+    def expert_pass(j0, j1, g0, last, hook):
         r0, count = j0 * blk, (j1 - j0) * blk
 
         def zero(i, carry):
@@ -206,12 +227,6 @@
             return carry
 
         lax.fori_loop(0, j1 - j0, zero, 0)
-
-        def gather(l):
-            row_pos = slot_r[pl.ds(l, 1), r0:r0 + count]
-            fan[:, 0:count] = jnp.where(row_pos == lax.broadcasted_iota(jnp.int32, (ecap, count), 0).astype(F32), 1.0, 0.0).astype(BF16)
-            for n in range(0, d_model, nt):
-                xin[:, n:n + nt] = dot(fan[:, 0:count], rows[r0:r0 + count, n:n + nt]).astype(BF16)
 
         def expert(l, carry):
             slot = l % 2
@@ -228,10 +243,10 @@
             for copy in weight_copies(l, slot):
                 copy.wait()
             for f in range(0, ffn, ft):
-                gate_act = dot(xin[...], wgb[slot, :, f:f + ft])
-                up_act = dot(xin[...], wub[slot, :, f:f + ft])
+                gate_act = dot(xin[l], wgb[slot, :, f:f + ft])
+                up_act = dot(xin[l], wub[slot, :, f:f + ft])
                 hid[:, f:f + ft] = (jax.nn.silu(gate_act) * up_act).astype(BF16)
-            gather((l + 1) % local)
+            gather((l + 1) % local, g0, j1, g0 != j0)
             lane = lax.broadcasted_iota(jnp.int32, (count, local), 1) == l
             pos = jnp.sum(jnp.where(lane, slot_c[r0:r0 + count, :], 0.0), axis=1, keepdims=True)
             gate = jnp.sum(jnp.where(lane, gate_c[r0:r0 + count, :], 0.0), axis=1, keepdims=True)
@@ -249,7 +264,7 @@
             spread(*held)
             return carry
 
-        gather(0)
+        gather(0, g0, j1, g0 != j0)
         lax.fori_loop(0, local, expert, 0)
 
         def finish(i, carry):
@@ -266,70 +281,73 @@
                 if (j, c) != (0, 0):
                     ret_copy(j, c).start()
 
+    def send_back(order):
+        for j in order:
+            for c in range(2):
+                if (j, c) != (0, 0):
+                    ret_copy(j, c).start()
+
     reset_base()
+    wait_sib_tables(0)
+    lax.fori_loop(0, 1, slot_tables, 0)
     own_tok.wait()
     wait_sib(0)
-    lax.fori_loop(0, 1, pack_slot, 0)
-    for j, dev in ((1, right), (2, left)):
-        relay_meta(j, j + 2, dev)
-    for sub in range(SUBS):
-        relay_sub(1, sub, 3, right)
-        relay_sub(2, sub, 4, left)
-    wait_sib(1)
-    wait_sib(2)
-    lax.fori_loop(1, first, pack_slot, 0)
+    lax.fori_loop(0, 1, pack_rows, 0)
+    for s in range(1, half - 1):
+        jr, jl = 2 * s - 1, 2 * s
+        relay_meta(jr, jr + 2, right)
+        relay_meta(jl, jl + 2, left)
+        wait_sib_tables(jr)
+        wait_sib_tables(jl)
+        lax.fori_loop(jr, jl + 1, slot_tables, 0)
+        for i in range(SUBS):
+            relay_sub(jr, i, jr + 2, right)
+            relay_sub(jl, swing(i), jl + 2, left)
+        wait_sib(jr)
+        wait_sib(jl)
+        lax.fori_loop(jr, jl + 1, pack_rows, 0)
+        if s == half - 3:
+            def early(l, carry):
+                gather(l, 0, jl + 1, False)
+                return carry
+
+            lax.fori_loop(0, local, early, 0)
+            reached = jl + 1
+
+    jr, jl = split, split + 1
 
     def hook_a(l):
         def meta_step():
-            relay_meta(3, 5, right)
-            relay_meta(4, 6, left)
-
-        def data_step(sub):
+            relay_meta(jr, far, right)
+            relay_meta(jl, None, left)
+
+        def data_step(i):
             def step():
-                relay_sub(3, sub, 5, right)
-                relay_sub(4, sub, 6, left)
+                relay_sub(jr, i, far if i < SUBS // 2 else None, right)
+                relay_sub(jl, swing(i), far if i < SUBS // 2 else None, left)
             return step
 
-        pl.when(l == 1)(meta_step)
-        for sub, at in enumerate((2, 4, 5, 7)):
-            pl.when(l == at)(data_step(sub))
-
-    expert_pass(0, first, False, hook_a)
+        pl.when(l == 0)(meta_step)
+        for i, at in enumerate((1, 2, 4, 5)):
+            pl.when(l == at)(data_step(i))
+
+    expert_pass(0, split, reached, False, hook_a)
     ret[0:cap, :] = rows[0:cap, :]
+    send_back(range(split - 1, -1, -1))
     reset_base()
-    wait_sib(3)
-    wait_sib(4)
-    lax.fori_loop(first, second, pack_slot, 0)
-
-    def hook_b(l):
-        def meta_step():
-            relay_meta(5, far, right)
-            relay_meta(6, None, left)
-
-        def data_step(sub):
-            def step():
-                relay_sub(5, sub, far if sub < SUBS // 2 else None, right)
-                relay_sub(6, sub, far if sub >= SUBS // 2 else None, left)
-            return step
-
-        pl.when(l == 0)(meta_step)
-        for sub, at in enumerate((1, 2, 4, 6)):
-            pl.when(l == at)(data_step(sub))
-        pl.when(l == 5)(lambda: send_back((1, 2, 0)))
-
-    expert_pass(first, second, False, hook_b)
-    send_back((3, 4))
-    reset_base()
-    wait_sib(5)
-    wait_sib(6)
-    lax.fori_loop(second, far, pack_slot, 0)
     relay_meta(far, None, right)
+    for j in range(split, nz):
+        wait_sib_tables(j)
+    lax.fori_loop(split, nz, slot_tables, 0)
+    wait_sib(jr)
+    wait_sib(jl)
+    lax.fori_loop(split, far, pack_rows, 0)
     for sub in range(SUBS):
         relay_sub(far, sub, None, right)
     wait_sib(far)
-    lax.fori_loop(far, nz, pack_slot, 0)
-    expert_pass(second, nz, True, lambda l: None)
-    send_back((7, 5, 6))
+    lax.fori_loop(far, nz, pack_rows, 0)
+    expert_pass(split, nz, split, True, lambda l: None)
+    send_back(range(nz - 1, split - 1, -1))
 
     near = split * blk
     for j in range(split):
@@ -373,7 +391,7 @@
         cap = tok_dev * (top_k // 2) // groups
         ecap = tok_dev * top_k // local
         row_count = groups * cap
-        most = 3 * 2 * cap
+        most = (2 * (nz // 2) - 3) * 2 * cap
         hbm = pl.BlockSpec(memory_space=pl.ANY)
         dma = pltpu.SemaphoreType.DMA
         return pl.pallas_call(
@@ -391,7 +409,7 @@
                 pltpu.VMEM((2, d_model, ffn), BF16),
                 pltpu.VMEM((2, d_model, ffn), BF16),
                 pltpu.VMEM((2, ffn, d_model), BF16),
-                pltpu.VMEM((ecap, d_model), BF16),
+                pltpu.VMEM((local, ecap, d_model), BF16),
                 pltpu.VMEM((ecap, ffn), BF16),
                 pltpu.VMEM((ecap, most), BF16),
                 pltpu.VMEM((most, ecap), BF16),
@@ -402,6 +420,7 @@
                 pltpu.VMEM((tok_dev, tok_dev), BF16),
                 pltpu.VMEM((local, 1), F32),
                 pltpu.VMEM((1, local), F32),
+                pltpu.VMEM((3, 2 * cap, 2 * tok_dev), BF16),
                 dma((nz, SUBS)), dma((nz, SUBS)), dma((nz, SUBS)), dma((nz, SUBS)),
                 dma((nz, 2)), dma((nz, 2)), dma((nz, 2)), dma((nz, 2)),
                 dma((nz, 2)), dma((nz, 2)), dma((2, 3)), dma((3,)),

time: 212 us -> 195 us (0.920)
  Pallas kernels: 209 us -> 193 us
    pallas_call x1, Pallas kernels: 209 us -> 193 us  [device_step(): pl.pallas_call(functools.partial(moe_kernel, groups), out_shape=jax.Shape...]
where the time goes in v5:
time: 195 us
  Pallas kernels  193 us (99%)
  local copies, waits for them, and re-layouts  2.3 us (1%)
    pallas_call x1, Pallas kernels, device_step(): pl.pallas_call(functools.partial(moe_kernel, groups), out_shape=jax.Shape...  193 us

profile of v5, /device:TPU:21, one launch (start us, length us, event | category | flops | bytes accessed | tf_op | source)
XLA Modules:
  0.0 195.0 jit_solution(3807370176784049720)
XLA Ops:
  0.0 192.7 %moe_fused.1 = bf16[256,2048]{1,0:T(8,128)(2,1)} custom-call(bf16[256,2048]{1,0:T(8,128)(2,1)} %tok.1, s32[8,256]{1,0:T(8,128)} %bitcast.2, f32[8,256]{1,0:T(8,128)} %bitcast.3, bf16[8,2048,768]{2,1,0:T(8,128)(2,1)} %w_gate.1, bf16[8,2048,768]{2,1,0:T(8,128)(2,1)} %w_up.1, bf16[8,768,2048]{2,1,0:T(8,128)(2,1)} %w_down.1), custom_call_target="tpu_custom_call" | custom-call | tf_op jit(solution)/shard_map/moe_fused/pallas_call | solution.py:397
  192.7 2.3 %copy.8 = bf16[256,2048]{1,0:T(8,128)(2,1)} copy(bf16[256,2048]{1,0:T(8,128)(2,1)} %moe_fused.1) | data formatting | bytes 2097152

commit v6 on v5

--- a/solution.py
+++ b/solution.py
@@ -25,9 +25,9 @@
     return lax.dot_general(a, b, (((0,), (0,)), ((), ())), preferred_element_type=F32)
 
 
-def moe_kernel(groups, tok, ids_in, gates_in, w_gate, w_up, w_down, out, xall, ids_all, gates_all, rows, acc, ret, wgb, wub, wdb, xin, hid, fan, fan_t,
-               slot_r, slot_c, gate_c, comb, tri, base_r, base_c, packs, ring_s, ring_r, sib_s, sib_r, mring_s, mring_r, msib_s, msib_r,
-               ret_s, ret_r, wsem, loc):
+def moe_kernel(groups, tok, ids_in, gates_in, w_gate, w_up, w_down, out, xall, ids_all, gates_all, rows, acc, total, ret, wgb, wub, wdb, xin, hid, fan, fan_t,
+               slot_r, slot_c, gate_c, comb, tri, base_r, base_c, packs, ship, sends, ring_s, ring_r, sib_s, sib_r, mring_s, mring_r, msib_s, msib_r,
+               far_s, far_r, ret_s, ret_r, wsem, dsem, loc):
     nz = groups // 2
     half = nz // 2
     tok_dev, d_model = tok.shape
@@ -37,7 +37,8 @@
     ecap = fan.shape[0]
     sub_rows = tok_dev // SUBS
     blk = 2 * cap
-    nt = min(512, d_model)
+    cuts = 4
+    nt = d_model // cuts
     ft = min(256, ffn)
     far = nz - 1
     split = 2 * half - 3
@@ -85,14 +86,32 @@
     def msib_copy(i, j):
         return remote(table_src(i, j, j == 0), tables[i][1].at[j, :, pl.ds(tok_dev, tok_dev)], msib_s.at[j, i], msib_r.at[j, i], sib)
 
-    def ret_copy(j, c):
-        off = j * blk + c * cap
-        return remote(rows.at[pl.ds(off, cap)], ret.at[pl.ds(off, cap)], ret_s.at[j, c], ret_r.at[j, c], device_at(source_shift(j), c))
+    def columns(m):
+        return pl.ds(pl.multiple_of(m * nt, nt), nt)
+
+    def ret_copy(j, c, m):
+        part = (pl.ds(j * blk + c * cap, cap), columns(m))
+        return remote(rows.at[part], ret.at[part], ret_s.at[j, c, m], ret_r.at[j, c, m], device_at(source_shift(j), c))
+
+    def far_copy(side, i):
+        j, c = ((split, 0), (split, 1), (far, 0))[i] if side == 0 else ((split + 1, 0), (split + 1, 1), (far, 1))[i]
+        shift = (1, 1, 2)[i] if side == 0 else (nz - 1, nz - 1, nz - 2)[i]
+        core = (0, 1, side)[i]
+        src = sends.at[side, pl.ds(i * cap, cap)]
+        return remote(src, rows.at[pl.ds(j * blk + c * cap, cap)], far_s.at[side, i], far_r.at[side, i], device_at(shift, core))
 
     def weight_copies(expert, slot):
         return (pltpu.make_async_copy(w_gate.at[expert], wgb.at[slot], wsem.at[slot, 0]),
-                pltpu.make_async_copy(w_up.at[expert], wub.at[slot], wsem.at[slot, 1]),
-                pltpu.make_async_copy(w_down.at[expert], wdb.at[slot], wsem.at[slot, 2]))
+                pltpu.make_async_copy(w_up.at[expert], wub.at[slot], wsem.at[slot, 1]))
+
+    def down_tile(l, bank):
+        if bank == 0:
+            return wdb.at[l // 4, :, pl.ds((l % 4) * nt, nt)]
+        buf = wgb if l < 4 else wub
+        return buf.at[(l % 4) // 2, pl.ds((l % 2) * ffn, ffn), pl.ds(0, nt)]
+
+    def down_copies(m, bank):
+        return [pltpu.make_async_copy(w_down.at[l, :, columns(m)], down_tile(l, bank), dsem.at[bank, l]) for l in range(local)]
 
     own_tok = pltpu.make_async_copy(tok, xall.at[0, pl.ds(0, tok_dev)], loc.at[0])
     own_tables = [pltpu.make_async_copy(tables[i][0], tables[i][1].at[0, :, pl.ds(0, tok_dev)], loc.at[1 + i]) for i in range(2)]
@@ -219,73 +238,97 @@
                 got = got + xin[l, :, n:n + nt].astype(F32)
             xin[l, :, n:n + nt] = got.astype(BF16)
 
-    def expert_pass(j0, j1, g0, last, hook):
+    def expert_pass(j0, j1, g0, hook, order):
         r0, count = j0 * blk, (j1 - j0) * blk
-
-        def zero(i, carry):
-            acc[pl.ds(pl.multiple_of(i * blk, blk), blk), :] = jnp.zeros((blk, d_model), F32)
-            return carry
-
-        lax.fori_loop(0, j1 - j0, zero, 0)
+        for copy in down_copies(0, 0):
+            copy.start()
+        gather(0, g0, j1, g0 != j0)
 
         def expert(l, carry):
             slot = l % 2
             hook(l)
 
             def prefetch():
-                for copy in weight_copies((l + 1) % local, (l + 1) % 2):
+                for copy in weight_copies(l + 1, (l + 1) % 2):
                     copy.start()
 
-            if last:
-                pl.when(l < local - 1)(prefetch)
-            else:
-                prefetch()
+            pl.when(l < local - 1)(prefetch)
             for copy in weight_copies(l, slot):
                 copy.wait()
             for f in range(0, ffn, ft):
                 gate_act = dot(xin[l], wgb[slot, :, f:f + ft])
                 up_act = dot(xin[l], wub[slot, :, f:f + ft])
-                hid[:, f:f + ft] = (jax.nn.silu(gate_act) * up_act).astype(BF16)
+                hid[l, :, f:f + ft] = (jax.nn.silu(gate_act) * up_act).astype(BF16)
             gather((l + 1) % local, g0, j1, g0 != j0)
             lane = lax.broadcasted_iota(jnp.int32, (count, local), 1) == l
             pos = jnp.sum(jnp.where(lane, slot_c[r0:r0 + count, :], 0.0), axis=1, keepdims=True)
-            gate = jnp.sum(jnp.where(lane, gate_c[r0:r0 + count, :], 0.0), axis=1, keepdims=True)
-            fan_t[0:count, :] = jnp.where(pos == lax.broadcasted_iota(jnp.int32, (count, ecap), 1).astype(F32), 1.0, 0.0).astype(BF16)
-
-            def spread(n, y):
-                acc[0:count, n:n + nt] += gate * dot(fan_t[0:count, :], y)
+            fan_t[l, 0:count, :] = jnp.where(pos == lax.broadcasted_iota(jnp.int32, (count, ecap), 1).astype(F32), 1.0, 0.0).astype(BF16)
+            return carry
+
+        lax.fori_loop(0, local, expert, 0)
+
+        def column(m, bank):
+            for copy in down_copies(m, bank):
+                copy.wait()
+
+            def spread(l, y):
+                part = gate_c[r0:r0 + count, l:l + 1] * dot(fan_t[l, 0:count, :], y)
+                if l == 0:
+                    acc[0:count, :] = part
+                else:
+                    acc[0:count, :] += part
 
             held = None
-            for n in range(0, d_model, nt):
-                y = dot(hid[...], wdb[slot, :, n:n + nt]).astype(BF16)
+            for l in range(local):
+                tile = wdb[l // 4, :, (l % 4) * nt:(l % 4 + 1) * nt] if bank == 0 else (wgb if l < 4 else wub)[(l % 4) // 2, (l % 2) * ffn:(l % 2 + 1) * ffn, 0:nt]
+                y = dot(hid[l], tile).astype(BF16)
                 if held is not None:
                     spread(*held)
-                held = (n, y)
+                held = (l, y)
             spread(*held)
+            rows[r0:r0 + count, columns(m)] = acc[0:count, :].astype(BF16)
+            if j0 == 0:
+                ret[0:cap, columns(m)] = acc[0:cap, :].astype(BF16)
+            for j in order:
+                for c in range(2):
+                    if (j, c) != (0, 0):
+                        ret_copy(j, c, m).start()
+
+        def two_columns(i, carry):
+            for copy in down_copies(2 * i + 1, 1):
+                copy.start()
+            column(2 * i, 0)
+
+            def prefetch():
+                for copy in down_copies(2 * i + 2, 0):
+                    copy.start()
+
+            pl.when(i < cuts // 2 - 1)(prefetch)
+            column(2 * i + 1, 1)
             return carry
 
-        gather(0, g0, j1, g0 != j0)
-        lax.fori_loop(0, local, expert, 0)
-
-        def finish(i, carry):
-            rows[pl.ds(pl.multiple_of(r0 + i * blk, blk), blk), :] = acc[pl.ds(pl.multiple_of(i * blk, blk), blk), :].astype(BF16)
-            return carry
-
-        lax.fori_loop(0, j1 - j0, finish, 0)
-
-    first, second = 3, split
-
-    def send_back(order):
-        for j in order:
-            for c in range(2):
-                if (j, c) != (0, 0):
-                    ret_copy(j, c).start()
-
-    def send_back(order):
-        for j in order:
-            for c in range(2):
-                if (j, c) != (0, 0):
-                    ret_copy(j, c).start()
+        lax.fori_loop(0, cuts // 2, two_columns, 0)
+
+    def ship_tables(side, j):
+        ids = ids_all[j, :, 0:tok_dev]
+        row_id = lax.broadcasted_iota(jnp.int32, (8, tok_dev), 0)
+        peers = [device_at(shift, core) for shift, core in (((1, 0), (1, 1), (2, 0)) if side == 0 else ((nz - 1, 0), (nz - 1, 1), (nz - 2, 1)))]
+        low = jnp.full((8, tok_dev), groups * local, jnp.int32)
+        for i, peer in enumerate(peers):
+            low = jnp.where(row_id == i, peer * local, low)
+        took = jnp.zeros((8, tok_dev), F32)
+        for i in range(top_k):
+            rel = ids[i:i + 1, :] - low
+            took = jnp.where((rel >= 0) & (rel < local), 1.0, took)
+        place = jnp.where(took > 0, dot(took.astype(BF16), tri[...]), -1.0)
+        for i in range(3):
+            ship[side, i * cap:(i + 1) * cap, :] = jnp.where(place[i:i + 1, :] == cap_iota, 1.0, 0.0).astype(BF16)
+
+    def ship_rows(side, j):
+        for n in range(0, d_model, nt):
+            sends[side, :, n:n + nt] = dot(ship[side], xall[j, 0:tok_dev, n:n + nt]).astype(BF16)
+        for i in range(3):
+            far_copy(side, i).start()
 
     reset_base()
     wait_sib_tables(0)
@@ -300,9 +343,16 @@
         wait_sib_tables(jr)
         wait_sib_tables(jl)
         lax.fori_loop(jr, jl + 1, slot_tables, 0)
+        onward = s < half - 2
+        if not onward:
+            ship_tables(0, jr)
+            ship_tables(1, jl)
         for i in range(SUBS):
-            relay_sub(jr, i, jr + 2, right)
-            relay_sub(jl, swing(i), jl + 2, left)
+            relay_sub(jr, i, jr + 2 if onward else None, right)
+            relay_sub(jl, swing(i), jl + 2 if onward else None, left)
+        if not onward:
+            ship_rows(0, jr)
+            ship_rows(1, jl)
         wait_sib(jr)
         wait_sib(jl)
         lax.fori_loop(jr, jl + 1, pack_rows, 0)
@@ -321,61 +371,53 @@
             relay_meta(jr, far, right)
             relay_meta(jl, None, left)
 
-        def data_step(i):
-            def step():
-                relay_sub(jr, i, far if i < SUBS // 2 else None, right)
-                relay_sub(jl, swing(i), far if i < SUBS // 2 else None, left)
-            return step
-
         pl.when(l == 0)(meta_step)
-        for i, at in enumerate((1, 2, 4, 5)):
-            pl.when(l == at)(data_step(i))
-
-    expert_pass(0, split, reached, False, hook_a)
-    ret[0:cap, :] = rows[0:cap, :]
-    send_back(range(split - 1, -1, -1))
+
+    expert_pass(0, split, reached, hook_a, range(split - 1, -1, -1))
+    for copy in weight_copies(0, 0):
+        copy.start()
     reset_base()
     relay_meta(far, None, right)
     for j in range(split, nz):
         wait_sib_tables(j)
     lax.fori_loop(split, nz, slot_tables, 0)
-    wait_sib(jr)
-    wait_sib(jl)
-    lax.fori_loop(split, far, pack_rows, 0)
-    for sub in range(SUBS):
-        relay_sub(far, sub, None, right)
-    wait_sib(far)
-    lax.fori_loop(far, nz, pack_rows, 0)
-    expert_pass(split, nz, split, True, lambda l: None)
-    send_back(range(nz - 1, split - 1, -1))
+    for side in range(2):
+        for i in range(3):
+            far_copy(side, i).wait_recv()
+    expert_pass(split, nz, split, lambda l: None, range(nz - 1, split - 1, -1))
 
     near = split * blk
-    for j in range(split):
-        for c in range(2):
-            if (j, c) != (0, 0):
-                ret_copy(j, c).wait_recv()
-
-    for n in range(0, d_model, nt):
-        acc[0:tok_dev, n:n + nt] = xall[0, 0:tok_dev, n:n + nt].astype(F32) + dot_tn(comb[0:near, :], ret[0:near, n:n + nt])
-    for j in range(split, nz):
-        for c in range(2):
-            ret_copy(j, c).wait_recv()
-
-    for n in range(0, d_model, nt):
-        out[:, n:n + nt] = (acc[0:tok_dev, n:n + nt] + dot_tn(comb[near:, :], ret[near:, n:n + nt])).astype(BF16)
-
+    for m in range(cuts):
+        for j in range(split):
+            for c in range(2):
+                if (j, c) != (0, 0):
+                    ret_copy(j, c, m).wait_recv()
+        n = m * nt
+        total[:, n:n + nt] = xall[0, 0:tok_dev, n:n + nt].astype(F32) + dot_tn(comb[0:near, :], ret[0:near, n:n + nt])
+    for m in range(cuts):
+        for j in range(split, nz):
+            for c in range(2):
+                ret_copy(j, c, m).wait_recv()
+        n = m * nt
+        out[:, n:n + nt] = (total[:, n:n + nt] + dot_tn(comb[near:, :], ret[near:, n:n + nt])).astype(BF16)
+
+    for side in range(2):
+        for i in range(3):
+            far_copy(side, i).wait_send()
     for j in range(nz):
         for i in range(2):
             msib_copy(i, j).wait_send()
             if j > 0:
                 mring_copy(i, 0, j, right).wait_send()
-        for sub in range(SUBS):
-            sib_copy(tok.at[sub_ds(sub)], j, sub).wait_send()
-            if j > 0:
-                ring_copy(tok.at[sub_ds(sub)], j, sub, right).wait_send()
+        if j < split:
+            for sub in range(SUBS):
+                sib_copy(tok.at[sub_ds(sub)], j, sub).wait_send()
+                if j > 0:
+                    ring_copy(tok.at[sub_ds(sub)], j, sub, right).wait_send()
         for c in range(2):
-            if (j, c) != (0, 0):
-                ret_copy(j, c).wait_send()
+            for m in range(cuts):
+                if (j, c) != (0, 0):
+                    ret_copy(j, c, m).wait_send()
 
 
 def solution(mesh):
@@ -400,19 +442,20 @@
             in_specs=[hbm] * 6,
             out_specs=pl.BlockSpec(memory_space=pltpu.VMEM),
             scratch_shapes=[
-                pltpu.VMEM((nz, 2 * tok_dev, d_model), BF16),
+                pltpu.VMEM((2 * (nz // 2) - 3, 2 * tok_dev, d_model), BF16),
                 pltpu.VMEM((nz, top_k, 2 * tok_dev), jnp.int32),
                 pltpu.VMEM((nz, top_k, 2 * tok_dev), F32),
                 pltpu.VMEM((row_count, d_model), BF16),
-                pltpu.VMEM((most, d_model), F32),
+                pltpu.VMEM((most, d_model // 4), F32),
+                pltpu.VMEM((tok_dev, d_model), F32),
                 pltpu.VMEM((row_count, d_model), BF16),
                 pltpu.VMEM((2, d_model, ffn), BF16),
                 pltpu.VMEM((2, d_model, ffn), BF16),
                 pltpu.VMEM((2, ffn, d_model), BF16),
                 pltpu.VMEM((local, ecap, d_model), BF16),
-                pltpu.VMEM((ecap, ffn), BF16),
+                pltpu.VMEM((local, ecap, ffn), BF16),
                 pltpu.VMEM((ecap, most), BF16),
-                pltpu.VMEM((most, ecap), BF16),
+                pltpu.VMEM((local, most, ecap), BF16),
                 pltpu.VMEM((local, row_count), F32),
                 pltpu.VMEM((row_count, local), F32),
                 pltpu.VMEM((row_count, local), F32),
@@ -421,9 +464,11 @@
                 pltpu.VMEM((local, 1), F32),
                 pltpu.VMEM((1, local), F32),
                 pltpu.VMEM((3, 2 * cap, 2 * tok_dev), BF16),
+                pltpu.VMEM((2, 3 * cap, tok_dev), BF16),
+                pltpu.VMEM((2, 3 * cap, d_model), BF16),
                 dma((nz, SUBS)), dma((nz, SUBS)), dma((nz, SUBS)), dma((nz, SUBS)),
                 dma((nz, 2)), dma((nz, 2)), dma((nz, 2)), dma((nz, 2)),
-                dma((nz, 2)), dma((nz, 2)), dma((2, 3)), dma((3,)),
+                dma((2, 3)), dma((2, 3)), dma((nz, 2, 4)), dma((nz, 2, 4)), dma((2, 2)), dma((2, local)), dma((3,)),
             ],
             compiler_params=pltpu.CompilerParams(collective_id=0, has_side_effects=True, vmem_limit_bytes=67043328),
             name='moe_fused',

time: 195 us -> 190 us (0.974)
  Pallas kernels: 193 us -> 188 us
    pallas_call x1, Pallas kernels: 193 us -> 188 us  [device_step(): pl.pallas_call(functools.partial(moe_kernel, groups), out_shape=jax.Shape...]
where the time goes in v6:
time: 190 us
  Pallas kernels  188 us (99%)
  local copies, waits for them, and re-layouts  2.3 us (1%)
    pallas_call x1, Pallas kernels, device_step(): pl.pallas_call(functools.partial(moe_kernel, groups), out_shape=jax.Shape...  188 us

profile of v6, /device:TPU:21, one launch (start us, length us, event | category | flops | bytes accessed | tf_op | source)
XLA Modules:
  0.0 189.9 jit_solution(17461666452550536935)
XLA Ops:
  0.0 187.6 %moe_fused.1 = bf16[256,2048]{1,0:T(8,128)(2,1)} custom-call(bf16[256,2048]{1,0:T(8,128)(2,1)} %tok.1, s32[8,256]{1,0:T(8,128)} %bitcast.2, f32[8,256]{1,0:T(8,128)} %bitcast.3, bf16[8,2048,768]{2,1,0:T(8,128)(2,1)} %w_gate.1, bf16[8,2048,768]{2,1,0:T(8,128)(2,1)} %w_up.1, bf16[8,768,2048]{2,1,0:T(8,128)(2,1)} %w_down.1), custom_call_target="tpu_custom_call" | custom-call | tf_op jit(solution)/shard_map/moe_fused/pallas_call | solution.py:439
  187.6 2.3 %copy.8 = bf16[256,2048]{1,0:T(8,128)(2,1)} copy(bf16[256,2048]{1,0:T(8,128)(2,1)} %moe_fused.1) | data formatting | bytes 2097152

commit v7 on v6

--- a/solution.py
+++ b/solution.py
@@ -25,7 +25,7 @@
     return lax.dot_general(a, b, (((0,), (0,)), ((), ())), preferred_element_type=F32)
 
 
-def moe_kernel(groups, tok, ids_in, gates_in, w_gate, w_up, w_down, out, xall, ids_all, gates_all, rows, acc, total, ret, wgb, wub, wdb, xin, hid, fan, fan_t,
+def moe_kernel(groups, tok, ids_in, gates_in, w_gate, w_up, w_down, out, xall, ids_all, gates_all, rows, acc, ret, wgb, wub, wdb, xin, hid, fan, fan_t,
                slot_r, slot_c, gate_c, comb, tri, base_r, base_c, packs, ship, sends, ring_s, ring_r, sib_s, sib_r, mring_s, mring_r, msib_s, msib_r,
                far_s, far_r, ret_s, ret_r, wsem, dsem, loc):
     nz = groups // 2
@@ -133,8 +133,9 @@
         ring_copy(tok.at[sub_ds(swing(i))], 2, swing(i), left).start()
     for sub in range(SUBS):
         sib_copy(tok.at[sub_ds(sub)], 0, sub).start()
-    for copy in weight_copies(0, 0):
-        copy.start()
+    for expert in range(3):
+        for copy in weight_copies(expert, (expert + 2) % 3):
+            copy.start()
 
     def relay_meta(j, next_j, dev):
         for i in range(2):
@@ -238,21 +239,27 @@
                 got = got + xin[l, :, n:n + nt].astype(F32)
             xin[l, :, n:n + nt] = got.astype(BF16)
 
-    def expert_pass(j0, j1, g0, hook, order):
+    def expert_pass(j0, j1, g0, last, hook, order):
         r0, count = j0 * blk, (j1 - j0) * blk
         for copy in down_copies(0, 0):
             copy.start()
         gather(0, g0, j1, g0 != j0)
 
         def expert(l, carry):
-            slot = l % 2
+            slot = (l + 2) % 3
             hook(l)
 
             def prefetch():
-                for copy in weight_copies(l + 1, (l + 1) % 2):
+                for copy in weight_copies(l + 2, (l + 1) % 3):
                     copy.start()
 
-            pl.when(l < local - 1)(prefetch)
+            def prefetch_next_pass():
+                for copy in weight_copies(0, 2):
+                    copy.start()
+
+            pl.when((l > 0) & (l < local - 2))(prefetch)
+            if not last:
+                pl.when(l == local - 1)(prefetch_next_pass)
             for copy in weight_copies(l, slot):
                 copy.wait()
             for f in range(0, ffn, ft):
@@ -373,9 +380,10 @@
 
         pl.when(l == 0)(meta_step)
 
-    expert_pass(0, split, reached, hook_a, range(split - 1, -1, -1))
-    for copy in weight_copies(0, 0):
-        copy.start()
+    expert_pass(0, split, reached, False, hook_a, range(split - 1, -1, -1))
+    for expert in (1, 2):
+        for copy in weight_copies(expert, expert - 1):
+            copy.start()
     reset_base()
     relay_meta(far, None, right)
     for j in range(split, nz):
@@ -384,22 +392,20 @@
     for side in range(2):
         for i in range(3):
             far_copy(side, i).wait_recv()
-    expert_pass(split, nz, split, lambda l: None, range(nz - 1, split - 1, -1))
-
-    near = split * blk
+    expert_pass(split, nz, split, True, lambda l: None, range(nz - 1, split - 1, -1))
+
     for m in range(cuts):
         for j in range(split):
             for c in range(2):
                 if (j, c) != (0, 0):
                     ret_copy(j, c, m).wait_recv()
-        n = m * nt
-        total[:, n:n + nt] = xall[0, 0:tok_dev, n:n + nt].astype(F32) + dot_tn(comb[0:near, :], ret[0:near, n:n + nt])
     for m in range(cuts):
         for j in range(split, nz):
             for c in range(2):
                 ret_copy(j, c, m).wait_recv()
         n = m * nt
-        out[:, n:n + nt] = (total[:, n:n + nt] + dot_tn(comb[near:, :], ret[near:, n:n + nt])).astype(BF16)
+        moe_sum = dot_tn(comb[...], ret[:, n:n + nt])
+        out[:, n:n + nt] = (xall[0, 0:tok_dev, n:n + nt].astype(F32) + moe_sum).astype(BF16)
 
     for side in range(2):
         for i in range(3):
@@ -447,10 +453,9 @@
                 pltpu.VMEM((nz, top_k, 2 * tok_dev), F32),
                 pltpu.VMEM((row_count, d_model), BF16),
                 pltpu.VMEM((most, d_model // 4), F32),
-                pltpu.VMEM((tok_dev, d_model), F32),
                 pltpu.VMEM((row_count, d_model), BF16),
-                pltpu.VMEM((2, d_model, ffn), BF16),
-                pltpu.VMEM((2, d_model, ffn), BF16),
+                pltpu.VMEM((3, d_model, ffn), BF16),
+                pltpu.VMEM((3, d_model, ffn), BF16),
                 pltpu.VMEM((2, ffn, d_model), BF16),
                 pltpu.VMEM((local, ecap, d_model), BF16),
                 pltpu.VMEM((local, ecap, ffn), BF16),
@@ -468,7 +473,7 @@
                 pltpu.VMEM((2, 3 * cap, d_model), BF16),
                 dma((nz, SUBS)), dma((nz, SUBS)), dma((nz, SUBS)), dma((nz, SUBS)),
                 dma((nz, 2)), dma((nz, 2)), dma((nz, 2)), dma((nz, 2)),
-                dma((2, 3)), dma((2, 3)), dma((nz, 2, 4)), dma((nz, 2, 4)), dma((2, 2)), dma((2, local)), dma((3,)),
+                dma((2, 3)), dma((2, 3)), dma((nz, 2, 4)), dma((nz, 2, 4)), dma((3, 2)), dma((2, local)), dma((3,)),
             ],
             compiler_params=pltpu.CompilerParams(collective_id=0, has_side_effects=True, vmem_limit_bytes=67043328),
             name='moe_fused',

time: 190 us -> 183 us (0.963)
  Pallas kernels: 188 us -> 180 us
    pallas_call x1, Pallas kernels: 188 us -> 180 us  [device_step(): pl.pallas_call(functools.partial(moe_kernel, groups), out_shape=jax.Shape...]
where the time goes in v7:
time: 183 us; the launch traced here: 182 us
  Pallas kernels  180 us (98%)
  local copies, waits for them, and re-layouts  2.3 us (1%)
    pallas_call x1, Pallas kernels, device_step(): pl.pallas_call(functools.partial(moe_kernel, groups), out_shape=jax.Shape...  180 us

profile of v7, /device:TPU:21, one launch (start us, length us, event | category | flops | bytes accessed | tf_op | source)
XLA Modules:
  0.0 182.2 jit_solution(10181152278240423996)
XLA Ops:
  0.0 179.9 %moe_fused.1 = bf16[256,2048]{1,0:T(8,128)(2,1)} custom-call(bf16[256,2048]{1,0:T(8,128)(2,1)} %tok.1, s32[8,256]{1,0:T(8,128)} %bitcast.2, f32[8,256]{1,0:T(8,128)} %bitcast.3, bf16[8,2048,768]{2,1,0:T(8,128)(2,1)} %w_gate.1, bf16[8,2048,768]{2,1,0:T(8,128)(2,1)} %w_up.1, bf16[8,768,2048]{2,1,0:T(8,128)(2,1)} %w_down.1), custom_call_target="tpu_custom_call" | custom-call | tf_op jit(solution)/shard_map/moe_fused/pallas_call | solution.py:445
  179.9 2.3 %copy.8 = bf16[256,2048]{1,0:T(8,128)(2,1)} copy(bf16[256,2048]{1,0:T(8,128)(2,1)} %moe_fused.1) | data formatting | bytes 2097152

commit v8 on v7

--- a/solution.py
+++ b/solution.py
@@ -25,7 +25,7 @@
     return lax.dot_general(a, b, (((0,), (0,)), ((), ())), preferred_element_type=F32)
 
 
-def moe_kernel(groups, tok, ids_in, gates_in, w_gate, w_up, w_down, out, xall, ids_all, gates_all, rows, acc, ret, wgb, wub, wdb, xin, hid, fan, fan_t,
+def moe_kernel(groups, tok, ids_in, gates_in, w_gate, w_up, w_down, ret, comb_out, xall, ids_all, gates_all, rows, acc, wgb, wub, wdb, xin, hid, fan, fan_t,
                slot_r, slot_c, gate_c, comb, tri, base_r, base_c, packs, ship, sends, ring_s, ring_r, sib_s, sib_r, mring_s, mring_r, msib_s, msib_r,
                far_s, far_r, ret_s, ret_r, wsem, dsem, loc):
     nz = groups // 2
@@ -93,6 +93,12 @@
         part = (pl.ds(j * blk + c * cap, cap), columns(m))
         return remote(rows.at[part], ret.at[part], ret_s.at[j, c, m], ret_r.at[j, c, m], device_at(source_shift(j), c))
 
+    def self_copy(m):
+        part = (pl.ds(0, cap), columns(m))
+        return pltpu.make_async_copy(rows.at[part], ret.at[part], ret_s.at[0, 0, m])
+
+    comb_copy = pltpu.make_async_copy(comb, comb_out, loc.at[3])
+
     def far_copy(side, i):
         j, c = ((split, 0), (split, 1), (far, 0))[i] if side == 0 else ((split + 1, 0), (split + 1, 1), (far, 1))[i]
         shift = (1, 1, 2)[i] if side == 0 else (nz - 1, nz - 1, nz - 2)[i]
@@ -120,9 +126,9 @@
     own_tok.start()
 
     barrier = pltpu.get_barrier_semaphore()
-    for step in range(1, groups):
-        pl.semaphore_signal(barrier, inc=1, device_id={'ep': (me + step) % groups}, device_id_type=MESH)
-    pl.semaphore_wait(barrier, groups - 1)
+    for peer in (right, left, sib):
+        pl.semaphore_signal(barrier, inc=1, device_id={'ep': peer}, device_id_type=MESH)
+    pl.semaphore_wait(barrier, 3)
 
     for i in range(2):
         mring_copy(i, 0, 1, right).start()
@@ -181,6 +187,7 @@
     for r in range(2 * nz):
         comb[r * cap:(r + 1) * cap, :] = jnp.where(rank[r:r + 1, :] == cap_iota, 1.0, 0.0).astype(BF16)
 
+    comb_copy.start()
     lo = me * local
 
     def reset_base():
@@ -295,7 +302,7 @@
             spread(*held)
             rows[r0:r0 + count, columns(m)] = acc[0:count, :].astype(BF16)
             if j0 == 0:
-                ret[0:cap, columns(m)] = acc[0:cap, :].astype(BF16)
+                self_copy(m).start()
             for j in order:
                 for c in range(2):
                     if (j, c) != (0, 0):
@@ -403,9 +410,8 @@
         for j in range(split, nz):
             for c in range(2):
                 ret_copy(j, c, m).wait_recv()
-        n = m * nt
-        moe_sum = dot_tn(comb[...], ret[:, n:n + nt])
-        out[:, n:n + nt] = (xall[0, 0:tok_dev, n:n + nt].astype(F32) + moe_sum).astype(BF16)
+        self_copy(m).wait()
+    comb_copy.wait()
 
     for side in range(2):
         for i in range(3):
@@ -442,18 +448,17 @@
         most = (2 * (nz // 2) - 3) * 2 * cap
         hbm = pl.BlockSpec(memory_space=pl.ANY)
         dma = pltpu.SemaphoreType.DMA
-        return pl.pallas_call(
+        returned, comb = pl.pallas_call(
             functools.partial(moe_kernel, groups),
-            out_shape=jax.ShapeDtypeStruct(tokens.shape, tokens.dtype),
+            out_shape=[jax.ShapeDtypeStruct((row_count, d_model), BF16), jax.ShapeDtypeStruct((row_count, tok_dev), BF16)],
             in_specs=[hbm] * 6,
-            out_specs=pl.BlockSpec(memory_space=pltpu.VMEM),
+            out_specs=[hbm] * 2,
             scratch_shapes=[
                 pltpu.VMEM((2 * (nz // 2) - 3, 2 * tok_dev, d_model), BF16),
                 pltpu.VMEM((nz, top_k, 2 * tok_dev), jnp.int32),
                 pltpu.VMEM((nz, top_k, 2 * tok_dev), F32),
                 pltpu.VMEM((row_count, d_model), BF16),
                 pltpu.VMEM((most, d_model // 4), F32),
-                pltpu.VMEM((row_count, d_model), BF16),
                 pltpu.VMEM((3, d_model, ffn), BF16),
                 pltpu.VMEM((3, d_model, ffn), BF16),
                 pltpu.VMEM((2, ffn, d_model), BF16),
@@ -473,10 +478,11 @@
                 pltpu.VMEM((2, 3 * cap, d_model), BF16),
                 dma((nz, SUBS)), dma((nz, SUBS)), dma((nz, SUBS)), dma((nz, SUBS)),
                 dma((nz, 2)), dma((nz, 2)), dma((nz, 2)), dma((nz, 2)),
-                dma((2, 3)), dma((2, 3)), dma((nz, 2, 4)), dma((nz, 2, 4)), dma((3, 2)), dma((2, local)), dma((3,)),
+                dma((2, 3)), dma((2, 3)), dma((nz, 2, 4)), dma((nz, 2, 4)), dma((3, 2)), dma((2, local)), dma((4,)),
             ],
             compiler_params=pltpu.CompilerParams(collective_id=0, has_side_effects=True, vmem_limit_bytes=67043328),
             name='moe_fused',
         )(tokens, expert_ids.T, gate_vals.T, w_gate, w_up, w_down)
+        return (tokens.astype(F32) + dot_tn(comb, returned)).astype(BF16)
 
     return jax.shard_map(device_step, mesh=mesh, in_specs=(row_spec, row_spec, row_spec, expert_spec, expert_spec, expert_spec), out_specs=row_spec, check_vma=False)

time: 183 us -> 182 us (level)
  matrix products: 0 us -> 4.89 us
  Pallas kernels: 180 us -> 176 us
  local copies, waits for them, and re-layouts: 2.3 us -> 0 us
    dot_general x0 -> x1, matrix products: none -> 4.89 us  [dot_tn(): lax.dot_general(a, b, (((0,), (0,)), ((), ())), preferred_element_type=F32)]
    pallas_call x1, Pallas kernels: 180 us -> 176 us  [device_step(): pl.pallas_call(functools.partial(moe_kernel, groups), out_shape=[jax.Shap...]
    unnamed x1 -> x0, local copies, waits for them, and re-layouts: 2.3 us -> none
where the time goes in v8:
time: 182 us; the launch traced here: 181 us
  Pallas kernels  176 us (97%)
  matrix products  4.89 us (3%)
    pallas_call x1, Pallas kernels, device_step(): pl.pallas_call(functools.partial(moe_kernel, groups), out_shape=[jax.Shap...  176 us
    dot_general x1, matrix products, dot_tn(): lax.dot_general(a, b, (((0,), (0,)), ((), ())), preferred_element_type=F32)  4.89 us

profile of v8, /device:TPU:21, one launch (start us, length us, event | category | flops | bytes accessed | tf_op | source)
XLA Modules:
  0.0 181.3 jit_solution(6593128161984177917)
XLA Ops:
  0.0 176.4 %moe_fused.1 = (bf16[1024,2048]{1,0:T(8,128)(2,1)}, bf16[1024,256]{1,0:T(8,128)(2,1)}) custom-call(bf16[256,2048]{1,0:T(8,128)(2,1)} %tok.1, s32[8,256]{1,0:T(8,128)} %bitcast.4, f32[8,256]{1,0:T(8,128)} %bitcast.5, bf16[8,2048,768]{2,1,0:T(8,128)(2,1)} %w_gate.1, bf16[8,2048,768]{2,1,0:T(8,128)(2,1)} %w_up.1, bf16[8,768,2048]{2,1,0:T(8,128)(2,1)} %w_down.1), custom_call_target="tpu_custom_call" | custom-call | tf_op jit(solution)/shard_map/moe_fused/pallas_call | solution.py:451
  176.4 4.9 %fusion = bf16[256,2048]{1,0:T(8,128)(2,1)} fusion(bf16[1024,256]{1,0:T(8,128)(2,1)} %get-tuple-element.7, bf16[1024,2048]{1,0:T(8,128)(2,1)} %get-tuple-element.8, bf16[256,2048]{1,0:T(8,128)(2,1)} %tok.1), kind=kOutput, calls=%fused_computation.1 | convolution fusion | flops 1075314688 | bytes 6815744 | tf_op jit(solution)/shard_map/dot_general | solution.py:25

commit v9 on v7

--- a/solution.py
+++ b/solution.py
@@ -27,7 +27,7 @@
 
 def moe_kernel(groups, tok, ids_in, gates_in, w_gate, w_up, w_down, out, xall, ids_all, gates_all, rows, acc, ret, wgb, wub, wdb, xin, hid, fan, fan_t,
                slot_r, slot_c, gate_c, comb, tri, base_r, base_c, packs, ship, sends, ring_s, ring_r, sib_s, sib_r, mring_s, mring_r, msib_s, msib_r,
-               far_s, far_r, ret_s, ret_r, wsem, dsem, loc):
+               far_s, far_r, ret_s, ret_r, wsem, dsem, loc, out_buf, out_sem):
     nz = groups // 2
     half = nz // 2
     tok_dev, d_model = tok.shape
@@ -93,6 +93,9 @@
         part = (pl.ds(j * blk + c * cap, cap), columns(m))
         return remote(rows.at[part], ret.at[part], ret_s.at[j, c, m], ret_r.at[j, c, m], device_at(source_shift(j), c))
 
+    def out_copy(m):
+        return pltpu.make_async_copy(out_buf.at[:, columns(m)], out.at[:, columns(m)], out_sem.at[m])
+
     def far_copy(side, i):
         j, c = ((split, 0), (split, 1), (far, 0))[i] if side == 0 else ((split + 1, 0), (split + 1, 1), (far, 1))[i]
         shift = (1, 1, 2)[i] if side == 0 else (nz - 1, nz - 1, nz - 2)[i]
@@ -120,9 +123,9 @@
     own_tok.start()
 
     barrier = pltpu.get_barrier_semaphore()
-    for step in range(1, groups):
-        pl.semaphore_signal(barrier, inc=1, device_id={'ep': (me + step) % groups}, device_id_type=MESH)
-    pl.semaphore_wait(barrier, groups - 1)
+    for peer in (right, left, sib):
+        pl.semaphore_signal(barrier, inc=1, device_id={'ep': peer}, device_id_type=MESH)
+    pl.semaphore_wait(barrier, 3)
 
     for i in range(2):
         mring_copy(i, 0, 1, right).start()
@@ -405,7 +408,8 @@
                 ret_copy(j, c, m).wait_recv()
         n = m * nt
         moe_sum = dot_tn(comb[...], ret[:, n:n + nt])
-        out[:, n:n + nt] = (xall[0, 0:tok_dev, n:n + nt].astype(F32) + moe_sum).astype(BF16)
+        out_buf[:, n:n + nt] = (xall[0, 0:tok_dev, n:n + nt].astype(F32) + moe_sum).astype(BF16)
+        out_copy(m).start()
 
     for side in range(2):
         for i in range(3):
@@ -424,6 +428,8 @@
             for m in range(cuts):
                 if (j, c) != (0, 0):
                     ret_copy(j, c, m).wait_send()
+    for m in range(cuts):
+        out_copy(m).wait()
 
 
 def solution(mesh):
@@ -446,7 +452,7 @@
             functools.partial(moe_kernel, groups),
             out_shape=jax.ShapeDtypeStruct(tokens.shape, tokens.dtype),
             in_specs=[hbm] * 6,
-            out_specs=pl.BlockSpec(memory_space=pltpu.VMEM),
+            out_specs=hbm,
             scratch_shapes=[
                 pltpu.VMEM((2 * (nz // 2) - 3, 2 * tok_dev, d_model), BF16),
                 pltpu.VMEM((nz, top_k, 2 * tok_dev), jnp.int32),
@@ -474,6 +480,7 @@
                 dma((nz, SUBS)), dma((nz, SUBS)), dma((nz, SUBS)), dma((nz, SUBS)),
                 dma((nz, 2)), dma((nz, 2)), dma((nz, 2)), dma((nz, 2)),
                 dma((2, 3)), dma((2, 3)), dma((nz, 2, 4)), dma((nz, 2, 4)), dma((3, 2)), dma((2, local)), dma((3,)),
+                pltpu.VMEM((tok_dev, d_model), BF16), dma((4,)),
             ],
             compiler_params=pltpu.CompilerParams(collective_id=0, has_side_effects=True, vmem_limit_bytes=67043328),
             name='moe_fused',

time: 183 us -> 181 us (0.989)
  Pallas kernels: 180 us -> 177 us
    pallas_call x1, Pallas kernels: 180 us -> 177 us  [device_step(): pl.pallas_call(functools.partial(moe_kernel, groups), out_shape=jax.Shape...]
where the time goes in v9:
time: 181 us; the launch traced here: 180 us
  Pallas kernels  177 us (98%)
  local copies, waits for them, and re-layouts  2.3 us (1%)
    pallas_call x1, Pallas kernels, device_step(): pl.pallas_call(functools.partial(moe_kernel, groups), out_shape=jax.Shape...  177 us

profile of v9, /device:TPU:21, one launch (start us, length us, event | category | flops | bytes accessed | tf_op | source)
XLA Modules:
  0.0 179.7 jit_solution(2742841680207679847)
XLA Ops:
  0.0 177.4 %moe_fused.1 = bf16[256,2048]{1,0:T(8,128)(2,1)} custom-call(bf16[256,2048]{1,0:T(8,128)(2,1)} %tok.1, s32[8,256]{1,0:T(8,128)} %bitcast.2, f32[8,256]{1,0:T(8,128)} %bitcast.3, bf16[8,2048,768]{2,1,0:T(8,128)(2,1)} %w_gate.1, bf16[8,2048,768]{2,1,0:T(8,128)(2,1)} %w_up.1, bf16[8,768,2048]{2,1,0:T(8,128)(2,1)} %w_down.1), custom_call_target="tpu_custom_call" | custom-call | tf_op jit(solution)/shard_map/moe_fused/pallas_call | solution.py:451
  177.4 2.3 %copy.8 = bf16[256,2048]{1,0:T(8,128)(2,1)} copy(bf16[256,2048]{1,0:T(8,128)(2,1)} %moe_fused.1) | data formatting | bytes 2097152
